TPU v7x, 8 devices: a whole 2x2x1 slice. The times are simulated.
8 devices in a mesh: dp: 1 (over z), ep: 8 (over y, x, core).
Axes of the slice: x: 2, y: 2, z: 1, core: 2. Of those that a mesh axis runs over, the one named last changes fastest.
Arguments:
- tokens: bfloat16 [512, 2048], P(('dp', 'ep'))
- route_idx: int32 [512, 6], P(('dp', 'ep'))
- gate_vals: float32 [512, 6], P(('dp', 'ep'))
- w_gate: bfloat16 [64, 2048, 1408], P('ep')
- w_up: bfloat16 [64, 2048, 1408], P('ep')
- w_down: bfloat16 [64, 1408, 2048], P('ep')
Outputs:
- output: bfloat16 [512, 2048], P(('dp', 'ep'))
All inputs are finite; a program needn't handle non-finite values.
Results may differ from a plain program's by a relative error of at most 0.00786066.
Values are sent between devices in bfloat16 or wider.
A program may use at most 1 GiB of HBM per device.

v0:
```python
import jax
import jax.numpy as jnp
from jax import lax
from jax.sharding import PartitionSpec as P


def pack_index(route_loc, n_experts, capacity):
    hit_mask = route_loc[:, :, None] == jnp.arange(n_experts)
    member = jnp.sum(hit_mask, axis=1, dtype=jnp.int32)
    running = jnp.cumsum(member, axis=0)
    targets = jnp.arange(capacity) + 1
    row_ids = jax.vmap(lambda column: jnp.searchsorted(column, targets, side="left"), in_axes=1)(running)
    slot_pos = jnp.take_along_axis(running, route_loc, axis=1) - 1
    return row_ids, slot_pos


def combine_rows(returned, flat_pos, gate_loc):
    picked = jnp.take(returned, flat_pos, axis=0)
    return jnp.sum(gate_loc[:, :, None] * picked.astype(jnp.float32), axis=1).astype(jnp.bfloat16)


def expert_ffn(rows_in, wg_loc, wu_loc, wd_loc):
    pre_gate = jnp.einsum("erd,edf->erf", rows_in, wg_loc, preferred_element_type=jnp.float32)
    pre_up = jnp.einsum("erd,edf->erf", rows_in, wu_loc, preferred_element_type=jnp.float32)
    hidden = (jax.nn.silu(pre_gate) * pre_up).astype(jnp.bfloat16)
    return jnp.einsum("erf,efd->erd", hidden, wd_loc, preferred_element_type=jnp.float32).astype(jnp.bfloat16)


def solution(mesh):
    group_n = mesh.shape["ep"]
    row_spec = P(("dp", "ep"))
    expert_spec = P("ep")

    def local_step(tok_loc, route_loc, gate_loc, wg_loc, wu_loc, wd_loc):
        local_n = wg_loc.shape[0]
        tok_dev, d_model = tok_loc.shape
        capacity = tok_dev // 2
        row_ids, slot_pos = pack_index(route_loc, local_n * group_n, capacity)
        row_ids = row_ids.reshape(group_n, local_n, capacity).transpose(1, 0, 2)
        send_buf = jnp.take(tok_loc, row_ids, axis=0, mode="fill", fill_value=0)
        recv_buf = lax.all_to_all(send_buf, "ep", 1, 1, tiled=True)
        expert_out = expert_ffn(recv_buf.reshape(local_n, group_n * capacity, d_model), wg_loc, wu_loc, wd_loc)
        returned = lax.all_to_all(expert_out.reshape(local_n, group_n, capacity, d_model), "ep", 1, 1, tiled=True)
        flat_pos = ((route_loc % local_n) * group_n + route_loc // local_n) * capacity + slot_pos
        return combine_rows(returned.reshape(-1, d_model), flat_pos, gate_loc)

    return jax.shard_map(local_step, mesh=mesh, in_specs=(row_spec, row_spec, row_spec, expert_spec, expert_spec, expert_spec), out_specs=row_spec, check_vma=False)
```

profile of v0, /device:TPU:0, one launch (start us, length us, event | category | flops | bytes accessed | tf_op | source)
XLA Modules:
  0.0 422.6 jit_solution(15292368480836039860)
XLA Ops:
  0.0 0.8 convert_reduce_fusion
  0.9 0.1 reduce_window_sum.11
  1.0 0.1 copy.58
  1.0 0.5 copy-done.2
  1.6 97.1 %while.24 = (s32[]{:T(128)}, u32[64,32]{1,0:T(8,128)S(1)}, u32[64,32]{1,0:T(8,128)S(1)}, s32[64,64]{1,0:T(8,128)S(1)}, s32[]{:T(128)}, /*index=5*/s32[]{:T(128)}) while((s32[]{:T(128)}, u32[64,32]{1,0:T(8,128)S(1)}, u32[64,32]{1,0:T(8,128)S(1)}, s32[64,64]{1,0:T(8,128)S(1)}, s32[]{:T(128)}, /*index=5*/s32[]{:T(128)}) %tuple.39), condition=%wide.region_3.4_spmd.clone, body=%wide.region_2.3_spmd.clone.sunk | while | flops 47139 | bytes 168273 | solution.py:12
  1.6 0.1 reshape.93
  1.7 13.6 %gather_fusion = s32[2048]{0:T(1024)S(1)} fusion(s32[64,64]{1,0:T(8,128)S(1)} %get-tuple-element.164, u32[2048]{0:T(1024)S(1)} %reshape.93), kind=kCustom, calls=%fused_computation.clone.clone.1 | custom fusion | bytes 32768 | tf_op jit(solution)/shard_map/vmap(jit(searchsorted))/vmap(jit(_searchsorted_scan_impl))/while/body/eval_jaxpr/gather | solution.py:12
  15.3 0.1 squeeze.8
  15.5 0.1 reshape.93
  15.5 13.6 %gather_fusion = s32[2048]{0:T(1024)S(1)} fusion(s32[64,64]{1,0:T(8,128)S(1)} %get-tuple-element.164, u32[2048]{0:T(1024)S(1)} %reshape.93), kind=kCustom, calls=%fused_computation.clone.clone.1 | custom fusion | bytes 32768 | tf_op jit(solution)/shard_map/vmap(jit(searchsorted))/vmap(jit(_searchsorted_scan_impl))/while/body/eval_jaxpr/gather | solution.py:12
  29.2 0.1 squeeze.8
  29.3 0.1 reshape.93
  29.4 13.6 %gather_fusion = s32[2048]{0:T(1024)S(1)} fusion(s32[64,64]{1,0:T(8,128)S(1)} %get-tuple-element.164, u32[2048]{0:T(1024)S(1)} %reshape.93), kind=kCustom, calls=%fused_computation.clone.clone.1 | custom fusion | bytes 32768 | tf_op jit(solution)/shard_map/vmap(jit(searchsorted))/vmap(jit(_searchsorted_scan_impl))/while/body/eval_jaxpr/gather | solution.py:12
  43.0 0.1 squeeze.8
  43.2 0.1 reshape.93
  43.3 13.6 %gather_fusion = s32[2048]{0:T(1024)S(1)} fusion(s32[64,64]{1,0:T(8,128)S(1)} %get-tuple-element.164, u32[2048]{0:T(1024)S(1)} %reshape.93), kind=kCustom, calls=%fused_computation.clone.clone.1 | custom fusion | bytes 32768 | tf_op jit(solution)/shard_map/vmap(jit(searchsorted))/vmap(jit(_searchsorted_scan_impl))/while/body/eval_jaxpr/gather | solution.py:12
  56.9 0.1 squeeze.8
  57.1 0.1 reshape.93
  57.2 13.6 %gather_fusion = s32[2048]{0:T(1024)S(1)} fusion(s32[64,64]{1,0:T(8,128)S(1)} %get-tuple-element.164, u32[2048]{0:T(1024)S(1)} %reshape.93), kind=kCustom, calls=%fused_computation.clone.clone.1 | custom fusion | bytes 32768 | tf_op jit(solution)/shard_map/vmap(jit(searchsorted))/vmap(jit(_searchsorted_scan_impl))/while/body/eval_jaxpr/gather | solution.py:12
  70.8 0.1 squeeze.8
  71.0 0.1 reshape.93
  71.0 13.6 %gather_fusion = s32[2048]{0:T(1024)S(1)} fusion(s32[64,64]{1,0:T(8,128)S(1)} %get-tuple-element.164, u32[2048]{0:T(1024)S(1)} %reshape.93), kind=kCustom, calls=%fused_computation.clone.clone.1 | custom fusion | bytes 32768 | tf_op jit(solution)/shard_map/vmap(jit(searchsorted))/vmap(jit(_searchsorted_scan_impl))/while/body/eval_jaxpr/gather | solution.py:12
  84.7 0.1 squeeze.8
  84.8 0.1 reshape.93
  84.9 13.6 %gather_fusion = s32[2048]{0:T(1024)S(1)} fusion(s32[64,64]{1,0:T(8,128)S(1)} %get-tuple-element.164, u32[2048]{0:T(1024)S(1)} %reshape.93), kind=kCustom, calls=%fused_computation.clone.clone.1 | custom fusion | bytes 32768 | tf_op jit(solution)/shard_map/vmap(jit(searchsorted))/vmap(jit(_searchsorted_scan_impl))/while/body/eval_jaxpr/gather | solution.py:12
  98.7 0.1 reshape.48
  98.8 11.0 %gather_fusion.1 = bf16[2048,2048]{1,0:T(8,128)(2,1)} fusion(bf16[64,2048]{1,0:T(8,128)(2,1)S(1)} %copy-done, s32[2048]{0:T(1024)S(1)} %broadcast_clamp_fusion), kind=kCustom, calls=%fused_computation.1 | custom fusion | bytes 16785408 | tf_op jit(solution)/shard_map/jit(_take)/gather | solution.py:40
  109.8 4.4 %copy_select_fusion = bf16[8,8,32,2048]{3,2,0,1:T(8,128)(2,1)S(1)} fusion(bf16[8,8,32,2048]{3,2,1,0:T(8,128)(2,1)} %bitcast.44, pred[8,8,32]{2,0,1:T(8,128)(4,1)S(1)} %copy.60), kind=kLoop, calls=%fused_computation.12 | loop fusion | flops 4194304 | bytes 16779264 | tf_op jit(solution)/shard_map/jit(_take)/select_n | solution.py:40
  114.2 98.1 %all_to_all.10 = bf16[8,8,32,2048]{3,2,0,1:T(8,128)(2,1)} all-to-all(bf16[8,8,32,2048]{3,2,0,1:T(8,128)(2,1)S(1)} %copy_select_fusion), channel_id=1, replica_groups=mesh['dp'=1,'ep'=8] {'ep'}, dimensions={1} | all-to-all | bytes 16777216 | tf_op jit(solution)/shard_map/all_to_all | solution.py:41
  212.3 8.3 %copy.62 = bf16[8,8,32,2048]{3,2,1,0:T(8,128)(2,1)} copy(bf16[8,8,32,2048]{3,2,0,1:T(8,128)(2,1)} %all_to_all.10) | data formatting | bytes 16777216 | tf_op jit(solution)/shard_map/all_to_all | solution.py:41
  220.6 30.5 %fusion.10 = f32[8,256,1408]{2,1,0:T(8,128)} fusion(bf16[8,256,2048]{2,1,0:T(8,128)(2,1)} %bitcast.45, bf16[8,2048,1408]{2,1,0:T(8,128)(2,1)} %param.11), kind=kOutput, calls=%fused_computation.40 | convolution fusion | flops 11811160064 | bytes 66060288 | tf_op jit(solution)/shard_map/erd,edf->erf/dot_general | solution.py:23
  251.1 41.6 %convolution_convert_fusion = bf16[8,256,2048]{2,1,0:T(8,128)(2,1)} fusion(bf16[8,1408,2048]{2,1,0:T(8,128)(2,1)} %param.13, f32[8,256,1408]{2,1,0:T(8,128)} %fusion.10, bf16[8,256,2048]{2,1,0:T(8,128)(2,1)} %bitcast.46, bf16[8,2048,1408]{2,1,0:T(8,128)(2,1)} %param.12), kind=kOutput, calls=%fused_computation.13 | convolution fusion | flops 23643815936 | bytes 120586240 | tf_op jit(solution)/shard_map/erf,efd->erd/dot_general | solution.py:26
  292.7 8.3 %copy.63 = bf16[8,8,32,2048]{3,2,0,1:T(8,128)(2,1)} copy(bf16[8,8,32,2048]{3,2,1,0:T(8,128)(2,1)} %bitcast.47) | data formatting | bytes 16777216 | tf_op jit(solution)/shard_map/reshape | solution.py:43
  301.1 4.0 all-to-all-start.1
  305.1 0.1 copy.55
  305.2 0.1 reshape.62
  305.3 2.9 gather_fusion.3
  308.2 0.1 reshape.65
  308.4 0.1 copy.56
  308.5 0.1 copy.65
  308.6 0.1 reshape.56
  308.7 0.1 copy.57
  308.8 0.1 copy.54
  308.9 89.9 %all-to-all-done.1 = bf16[8,8,32,2048]{3,2,0,1:T(8,128)(2,1)} async-done(((bf16[8,8,32,2048]{3,2,0,1:T(8,128)(2,1)}), bf16[8,8,32,2048]{3,2,0,1:T(8,128)(2,1)}, u32[]{:S(2)}, u32[]{:S(2)}) %all-to-all-start.1) | async-done | bytes 8388640 | tf_op jit(solution)/shard_map/all_to_all | solution.py:43
  398.9 8.3 %copy.64 = bf16[8,8,32,2048]{3,2,1,0:T(8,128)(2,1)} copy(bf16[8,8,32,2048]{3,2,0,1:T(8,128)(2,1)} %all-to-all-done.1) | data formatting | bytes 16777216 | tf_op jit(solution)/shard_map/all_to_all | solution.py:43
  407.1 8.9 %gather_fusion.2 = bf16[384,2048]{1,0:T(8,128)(2,1)S(1)} fusion(bf16[2048,2048]{1,0:T(8,128)(2,1)} %bitcast.43, s32[1024]{0:T(1024)S(1)} %pad_clamp_fusion), kind=kCustom, calls=%fused_computation.2 | custom fusion | bytes 3147264 | tf_op jit(solution)/shard_map/jit(_take)/gather | solution.py:18
  416.0 1.6 reshape.55
  417.7 4.9 %multiply_reduce_fusion = bf16[64,2048]{1,0:T(8,128)(2,1)} fusion(bf16[64,6,2048]{2,1,0:T(8,128)(2,1)} %reshape.55, f32[64,6]{1,0:T(8,128)S(1)} %copy.54, pred[64,6]{1,0:T(8,128)(4,1)S(1)} %copy.57), kind=kLoop, calls=%fused_computation.14 | loop fusion | flops 3014656 | bytes 1836928 | tf_op jit(solution)/shard_map/reduce_sum | solution.py:19
  (57 shorter events, 0.6 us)
Async XLA Ops:
  0.0 98.8 %copy-start = (bf16[64,2048]{1,0:T(8,128)(2,1)S(1)}, bf16[64,2048]{1,0:T(8,128)(2,1)}, u32[]{:S(2)}) copy-start(bf16[64,2048]{1,0:T(8,128)(2,1)} %param.8) | copy-start | bytes 786436
  1.0 0.6 copy-start.2
  301.1 4.0 copy-start.4
  301.1 4.3 %copy-start.3 = (s32[64,64]{1,0:T(8,128)S(1)}, s32[64,64]{1,0:T(8,128)}, u32[]{:S(2)}) copy-start(s32[64,64]{1,0:T(8,128)} %copy-done.2) | copy-start | bytes 49156
  301.1 97.8 %all-to-all-start.1 = ((bf16[8,8,32,2048]{3,2,0,1:T(8,128)(2,1)}), bf16[8,8,32,2048]{3,2,0,1:T(8,128)(2,1)}, u32[]{:S(2)}, u32[]{:S(2)}) async-start(bf16[8,8,32,2048]{3,2,0,1:T(8,128)(2,1)} %copy.63), calls=%async_computation.1 | async-start | bytes 16777216 | tf_op jit(solution)/shard_map/all_to_all | solution.py:43
  305.3 3.5 copy-start.5
  407.1 15.4 %copy-start.1 = (bf16[64,2048]{1,0:T(8,128)(2,1)S(1)}, bf16[64,2048]{1,0:T(8,128)(2,1)}, u32[]{:S(2)}) copy-start(bf16[64,2048]{1,0:T(8,128)(2,1)} %param.8) | copy-start | bytes 786436
where the time goes:
time: 423 us
  local copies, waits for them, and re-layouts  147 us (35%)
  blocking collectives  98.1 us (23%)
  waiting for transfers between devices  89.9 us (21%)
  matrix products  72.1 us (17%)
  other arithmetic  10.8 us (3%)
    all_to_all x1, blocking collectives, local_step(): recv_buf = lax.all_to_all(send_buf, 'ep', 1, 1, tiled=True)  98.1 us
    gather x14, local copies, waits for them, and re-layouts, pack_index(): jnp.searchsorted(column, targets, side='left')  95.8 us
    all_to_all x1, waiting for transfers between devices, local_step(): lax.all_to_all(expert_out.reshape(local_n, group_n, capacity, d_model), '...  89.9 us
    dot_general x1, matrix products, expert_ffn(): jnp.einsum('erf,efd->erd', hidden, wd_loc, preferred_element_type=jnp.flo...  41.6 us
    dot_general x1, matrix products, expert_ffn(): jnp.einsum('erd,edf->erf', rows_in, wg_loc, preferred_element_type=jnp.fl...  30.5 us
    gather x1, local copies, waits for them, and re-layouts, local_step(): send_buf = jnp.take(tok_loc, row_ids, axis=0, mode='fill', fill_value=0)  11 us
    gather x2, local copies, waits for them, and re-layouts, combine_rows(): picked = jnp.take(returned, flat_pos, axis=0)  10.5 us
  transfers between devices with their start and end apart: 1, of which 1 were waited for; matrix products, arithmetic and copies ran while one was open for 1% of the time, Pallas kernels for 0%

commit v1 on v0

v1 whole, which is shorter than its diff:
```python
import jax
import jax.numpy as jnp
from jax import lax
from jax.experimental import pallas as pl
from jax.experimental.pallas import tpu as pltpu
from jax.sharding import PartitionSpec as P

BF16 = jnp.bfloat16
F32 = jnp.float32
MESH = pl.DeviceIdType.MESH
N_DEV = 8
CAP = 32
SLOTS = 3
COLS = 256
VMEM = pl.BlockSpec(memory_space=pltpu.VMEM)
ANY = pl.BlockSpec(memory_space=pl.ANY)


def remote(src, dst, send_sem, recv_sem, peer):
    return pltpu.make_async_remote_copy(src_ref=src, dst_ref=dst, send_sem=send_sem, recv_sem=recv_sem, device_id={"ep": peer}, device_id_type=MESH)


def on_chip(shape, dtype):
    return pltpu.VMEM(shape, dtype)


def pin(v):
    return pltpu.with_memory_space_constraint(v, pltpu.VMEM)


def place():
    me = lax.axis_index("ep")
    core = lax.rem(me, 2)
    x = lax.rem(me // 2, 2)
    y = me // 4
    return me, core, x, y, me + 1 - 2 * core, me + 2 - 4 * x, me + 4 - 8 * y


def entry_barrier(me):
    barrier = pltpu.get_barrier_semaphore()
    for d in range(1, N_DEV):
        pl.semaphore_signal(barrier, inc=1, device_id={"ep": lax.rem(me + d, N_DEV)}, device_id_type=MESH)
    pl.semaphore_wait(barrier, N_DEV - 1)


def gather_kernel(tok, route_t, gate_t, wg, wu, w_out, x_out, sg_out, h_out, s_out, wd_out, pad, sg_loc, w_sem, sib_s, sib_r, link_s, link_r, sg_s, sg_r):
    me, core, x, y, sib, xn, yn = place()
    loads = []
    for e in range(SLOTS):
        loads.append(pltpu.make_async_copy(wg.at[e], w_out.at[e, 0], w_sem.at[e, 0]))
        loads.append(pltpu.make_async_copy(wu.at[e], w_out.at[e, 1], w_sem.at[e, 1]))
    for load in loads:
        load.start()
    entry_barrier(me)

    n_tok = tok.shape[0]
    half = n_tok // 2
    first, second = pl.ds(0, half), pl.ds(half, half)

    def rows(device, part=0, count=half):
        return x_out.at[pl.ds(pl.multiple_of(device * n_tok + part * half, half), count)]

    to_x_a = remote(tok.at[first], rows(me, 0), link_s.at[0], link_r.at[0], xn)
    to_x_b = remote(tok.at[second], rows(me, 1), link_s.at[1], link_r.at[1], xn)
    to_y_b = remote(tok.at[second], rows(me, 1), link_s.at[2], link_r.at[2], yn)
    to_y_a = remote(tok.at[first], rows(me, 0), link_s.at[3], link_r.at[3], yn)
    to_sib = remote(tok, rows(me, 0, n_tok), sib_s.at[0], sib_r.at[0], sib)
    for copy in (to_x_a, to_y_b, to_x_b, to_y_a, to_sib):
        copy.start()

    pad[...] = jnp.zeros_like(pad)
    pad[0, 0:6, 0:n_tok] = route_t[...].astype(F32)
    pad[1, 0:6, 0:n_tok] = gate_t[...]
    routes = pad[0] + pltpu.roll(pad[0], n_tok, 1)
    gates = pad[1] + pltpu.roll(pad[1], n_tok, 1)
    expert = lax.broadcasted_iota(jnp.int32, (64, 128), 0).astype(F32)
    lane = lax.broadcasted_iota(jnp.int32, (64, 128), 1)
    mine = (lane // n_tok) == core
    member = jnp.zeros((64, 128), F32)
    weight = jnp.zeros((64, 128), F32)
    for k in range(6):
        hit = (expert == routes[k : k + 1, :]) & mine
        member = jnp.where(hit, 1.0, member)
        weight = jnp.where(hit, gates[k : k + 1, :], weight)
    row = lax.broadcasted_iota(jnp.int32, (128, 128), 0)
    col = lax.broadcasted_iota(jnp.int32, (128, 128), 1)
    upto = jnp.where((row <= col), 1.0, 0.0).astype(BF16)
    rank = jnp.dot(member.astype(BF16), upto, preferred_element_type=F32)
    code = jnp.where(member > 0.5, rank + (me * CAP).astype(F32), 0.0)
    sg_loc[:, 0:8, :] = code.reshape(8, 8, 128)
    sg_loc[:, 8:16, :] = weight.reshape(8, 8, 128)
    sg_out[me] = sg_loc[me]
    sg_copies = []
    for d in range(1, N_DEV):
        peer = lax.rem(me + d, N_DEV)
        sg_copies.append(remote(sg_loc.at[peer], sg_out.at[me], sg_s.at[d], sg_r.at[d], peer))
    x_out[pl.ds(pl.multiple_of(me * n_tok, n_tok), n_tok), :] = tok[...]
    for copy in sg_copies:
        copy.start()

    dg = lax.rem(xn + 4, N_DEV)
    passed = []

    def pass_on(index, source, part):
        copy = remote(rows(source, part), rows(source, part), sib_s.at[index], sib_r.at[index], sib)
        copy.start()
        passed.append(copy)

    to_x_a.wait_recv()
    via_y = remote(rows(xn, 0), rows(xn, 0), link_s.at[4], link_r.at[4], yn)
    via_y.start()
    pass_on(1, xn, 0)
    to_y_b.wait_recv()
    via_x = remote(rows(yn, 1), rows(yn, 1), link_s.at[5], link_r.at[5], xn)
    via_x.start()
    pass_on(2, yn, 1)
    to_x_b.wait_recv()
    pass_on(3, xn, 1)
    to_y_a.wait_recv()
    pass_on(4, yn, 0)
    via_y.wait_recv()
    pass_on(5, dg, 0)
    via_x.wait_recv()
    pass_on(6, dg, 1)
    for copy in (to_x_a, to_x_b, to_y_b, to_y_a, via_y, via_x):
        copy.wait_send()
    to_sib.wait()
    for copy in passed + sg_copies:
        copy.wait()
    for load in loads:
        load.wait()


def hidden_kernel(w_in, h_in, s_in, wd_in, x_all, sg, wg, wu, wd, w_buf, h_out, s_out, wd_out, codes, xe, w_sem, d_sem):
    n_exp = wg.shape[0]
    d_ff = wg.shape[2]
    down = pltpu.make_async_copy(wd.at[:, :, pl.ds(0, COLS)], wd_out.at[0], d_sem)
    down.start()
    for p in range(4):
        codes[:, pl.ds(p * 128, 128)] = sg[2 * p, 0:8, :] + sg[2 * p + 1, 0:8, :]

    def load(e, part, src):
        s = lax.rem(e, SLOTS)
        return pltpu.make_async_copy(src.at[e], w_buf.at[s, part], w_sem.at[s, part])

    def hidden_rows(e, cap, slot):
        m = cap * N_DEV
        r = lax.broadcasted_iota(jnp.int32, (m, 512), 0)
        target = ((r // cap) * CAP + lax.rem(r, cap) + 1).astype(F32)
        pick = (target == codes[pl.ds(e, 1), :]).astype(BF16)
        for c in range(0, x_all.shape[1], 512):
            part = jnp.dot(pick, x_all[:, pl.ds(c, 512)], preferred_element_type=F32)
            xe[pl.ds(0, m), pl.ds(c, 512)] = part.astype(BF16)

        def put(act, c, w):
            if cap == CAP:
                h_out[e, :, pl.ds(c, w)] = act
            else:
                for i in range(N_DEV):
                    h_out[e, pl.ds(i * CAP, cap), pl.ds(c, w)] = act[i * cap : (i + 1) * cap]
                    h_out[e, pl.ds(i * CAP + cap, CAP - cap), pl.ds(c, w)] = jnp.zeros((CAP - cap, w), BF16)

        def act_of(a, b):
            return (a * jax.nn.sigmoid(a) * b).astype(BF16)

        rows = xe[pl.ds(0, m), :]
        for c in range(0, d_ff - 128, 256):
            a = jnp.dot(rows, w_buf[slot, 0, :, pl.ds(c, 256)], preferred_element_type=F32)
            b = jnp.dot(rows, w_buf[slot, 1, :, pl.ds(c, 256)], preferred_element_type=F32)
            put(act_of(a, b), c, 256)
        c = d_ff - 128
        both = jnp.concatenate([w_buf[slot, 0, :, pl.ds(c, 128)], w_buf[slot, 1, :, pl.ds(c, 128)]], axis=1)
        ab = jnp.dot(rows, both, preferred_element_type=F32)
        put(act_of(ab[:, :128], ab[:, 128:]), c, 128)

    def step(e, carry):
        slot = lax.rem(e, SLOTS)

        @pl.when(e >= SLOTS)
        def _():
            load(e, 0, wg).wait()
            load(e, 1, wu).wait()

        code_row = codes[pl.ds(e, 1), :]
        block = lax.broadcasted_iota(jnp.int32, (1, 512), 1) // 64
        most = jnp.max(code_row - (block * CAP).astype(F32))
        small = most <= 16.0

        @pl.when(small)
        def _():
            hidden_rows(e, CAP // 2, slot)

        @pl.when(jnp.logical_not(small))
        def _():
            hidden_rows(e, CAP, slot)

        @pl.when(e + SLOTS < n_exp)
        def _():
            load(e + SLOTS, 0, wg).start()
            load(e + SLOTS, 1, wu).start()

        return carry

    lax.fori_loop(0, n_exp, step, 0)

    r = lax.broadcasted_iota(jnp.int32, (256, 128), 0)
    lane = lax.broadcasted_iota(jnp.int32, (256, 128), 1)
    for p in range(4):
        target = ((2 * p + lane // 64) * CAP + lax.rem(r, CAP) + 1).astype(F32)
        code = sg[2 * p, 0:8, :] + sg[2 * p + 1, 0:8, :]
        gate = sg[2 * p, 8:16, :] + sg[2 * p + 1, 8:16, :]
        code = jnp.broadcast_to(code[:, None, :], (8, CAP, 128)).reshape(256, 128)
        gate = jnp.broadcast_to(gate[:, None, :], (8, CAP, 128)).reshape(256, 128)
        s_t = jnp.where(code == target, gate, 0.0)
        s_f = s_t.T
        hi = jnp.minimum(s_f, 3.3895e38).astype(BF16)
        rest = s_f - hi.astype(F32)
        mid = rest.astype(BF16)
        low = (rest - mid.astype(F32)).astype(BF16)
        s_out[p, 0] = hi
        s_out[p, 1] = mid
        s_out[p, 2] = low
    down.wait()


def combine_kernel(wd_in, h, s, wd, wd_buf, y_out, o, part, d2d, h1a, h1b, h2a, h2b, w_sem, ds, dr, h1as, h1ar, h1bs, h1br, h2as, h2ar, h2bs, h2br):
    me, core, x, y, sib, xn, yn = place()
    n_blk = wd.shape[2] // COLS
    half = 32
    first, second = pl.ds(0, half), pl.ds(half, half)

    def load(b):
        s_ = lax.rem(b, 2)
        return pltpu.make_async_copy(wd.at[:, :, pl.ds(pl.multiple_of(b * COLS, COLS), COLS)], wd_buf.at[s_], w_sem.at[s_])

    load(1).start()
    entry_barrier(me)

    def send_d2d(b):
        return remote(part.at[b, 1 - core], d2d.at[b], ds.at[b], dr.at[b], sib)

    def send_1a(b):
        return remote(part.at[b, core, :, 1 - x, first], h1a.at[b], h1as.at[b], h1ar.at[b], xn)

    def send_1b(b):
        return remote(part.at[b, core, 1 - y, :, second], h1b.at[b], h1bs.at[b], h1br.at[b], yn)

    def send_2a(b):
        return remote(part.at[b, core, 1 - y, x, first], h2a.at[b], h2as.at[b], h2ar.at[b], yn)

    def send_2b(b):
        return remote(part.at[b, core, y, 1 - x, second], h2b.at[b], h2bs.at[b], h2br.at[b], xn)

    def lag(b, k, body):
        @pl.when((b >= k) & (b < n_blk + k))
        def _():
            body(b - k)

    def stage_1(b):
        send_d2d(b).start()

    def stage_2(b):
        send_d2d(b).wait_recv()
        part[b, core] += d2d[b]
        send_1a(b).start()
        send_1b(b).start()

    def stage_3(b):
        send_1a(b).wait_recv()
        send_1b(b).wait_recv()
        part[b, core, :, x, first] += h1a[b]
        part[b, core, y, :, second] += h1b[b]
        send_2a(b).start()
        send_2b(b).start()

    def stage_4(b):
        send_2a(b).wait_recv()
        send_2b(b).wait_recv()
        cols = pl.ds(pl.multiple_of(b * COLS, COLS), COLS)
        y_out[first, cols] = (part[b, core, y, x, first] + h2a[b]).astype(BF16)
        y_out[second, cols] = (part[b, core, y, x, second] + h2b[b]).astype(BF16)

    def compute(b):
        slot = lax.rem(b, 2)

        @pl.when((b >= 1) & (b + 1 < n_blk))
        def _():
            load(b + 1).start()

        @pl.when(b >= 1)
        def _():
            load(b).wait()

        for e in range(h.shape[0]):
            out = jnp.dot(h[e], wd_buf[slot, e], preferred_element_type=F32).astype(BF16)
            for i in range(N_DEV):
                o[i, pl.ds(e * CAP, CAP), :] = out[i * CAP : (i + 1) * CAP]
        for i in range(N_DEV):
            gates = s[i // 2, :, pl.ds((i % 2) * 64, 64), :].reshape(192, 256)
            terms = jnp.dot(gates, o[i], preferred_element_type=F32)
            part[b, i % 2, i // 4, (i // 2) % 2] = terms[0:64] + terms[64:128] + terms[128:192]

    def step(b, carry):
        lag(b, 1, stage_1)
        lag(b, 2, stage_2)
        lag(b, 3, stage_3)
        lag(b, 4, stage_4)
        lag(b, 0, compute)
        return carry

    lax.fori_loop(0, n_blk + 4, step, 0)

    def drain(b, carry):
        for send in (send_d2d, send_1a, send_1b, send_2a, send_2b):
            send(b).wait_send()
        return carry

    lax.fori_loop(0, n_blk, drain, 0)


def solution(mesh):
    row_spec = P(("dp", "ep"))
    expert_spec = P("ep")
    dma = pltpu.SemaphoreType.DMA

    def local_step(tok, route, gate, wg, wu, wd):
        n_exp, d_model, d_ff = wg.shape
        n_tok = tok.shape[0]
        n_blk = d_model // COLS
        w_on, x_all, sg, h, s, wd_on = pl.pallas_call(
            gather_kernel,
            out_shape=[on_chip((SLOTS, 2, d_model, d_ff), BF16), on_chip((N_DEV * n_tok, d_model), BF16), on_chip((N_DEV, 16, 128), F32), on_chip((n_exp, N_DEV * CAP, d_ff), BF16), on_chip((4, 3, 128, 256), BF16), on_chip((2, n_exp, d_ff, COLS), BF16)],
            in_specs=[VMEM, VMEM, VMEM, ANY, ANY],
            out_specs=[VMEM] * 6,
            scratch_shapes=[pltpu.VMEM((2, 8, 128), F32), pltpu.VMEM((N_DEV, 16, 128), F32), dma((SLOTS, 2)), dma((7,)), dma((7,)), dma((6,)), dma((6,)), dma((N_DEV,)), dma((N_DEV,))],
            compiler_params=pltpu.CompilerParams(collective_id=0, has_side_effects=True, vmem_limit_bytes=6 << 20),
            name="gather",
        )(tok, route.T, gate.T, wg, wu)
        unused, h, s, wd_on = pl.pallas_call(
            hidden_kernel,
            out_shape=[on_chip(w_on.shape, BF16), on_chip((n_exp, N_DEV * CAP, d_ff), BF16), on_chip((4, 3, 128, 256), BF16), on_chip((2, n_exp, d_ff, COLS), BF16)],
            in_specs=[VMEM] * 6 + [ANY] * 3,
            out_specs=[VMEM] * 4,
            scratch_shapes=[pltpu.VMEM((8, 512), F32), pltpu.VMEM((256, d_model), BF16), dma((SLOTS, 2)), dma],
            input_output_aliases={0: 0, 1: 1, 2: 2, 3: 3},
            compiler_params=pltpu.CompilerParams(vmem_limit_bytes=6 << 20),
            name="hidden",
        )(pin(w_on), pin(h), pin(s), pin(wd_on), pin(x_all), pin(sg), wg, wu, wd)
        out = pl.pallas_call(
            combine_kernel,
            out_shape=[on_chip(wd_on.shape, BF16), jax.ShapeDtypeStruct((n_tok, d_model), BF16)],
            in_specs=[VMEM, VMEM, VMEM, ANY],
            out_specs=[VMEM] * 2,
            scratch_shapes=[
                pltpu.VMEM((N_DEV, 256, COLS), BF16),
                pltpu.VMEM((n_blk, 2, 2, 2, n_tok, COLS), F32),
                pltpu.VMEM((n_blk, 2, 2, n_tok, COLS), F32),
                pltpu.VMEM((n_blk, 2, n_tok // 2, COLS), F32),
                pltpu.VMEM((n_blk, 2, n_tok // 2, COLS), F32),
                pltpu.VMEM((n_blk, n_tok // 2, COLS), F32),
                pltpu.VMEM((n_blk, n_tok // 2, COLS), F32),
                dma((2,)),
            ]
            + [dma((n_blk,))] * 10,
            input_output_aliases={0: 0},
            compiler_params=pltpu.CompilerParams(collective_id=1, has_side_effects=True, vmem_limit_bytes=16 << 20),
            name="combine",
        )(pin(wd_on), pin(h), pin(s), wd)
        return out[1]

    return jax.shard_map(local_step, mesh=mesh, in_specs=(row_spec, row_spec, row_spec, expert_spec, expert_spec, expert_spec), out_specs=row_spec, check_vma=False)
```

time: 423 us -> 74.8 us (0.18)
  local copies, waits for them, and re-layouts: 147 us -> 0.71 us
  blocking collectives: 98.1 us -> 0 us
  waiting for transfers between devices: 89.9 us -> 0 us
  Pallas kernels: 0 us -> 73.8 us
  matrix products: 72.1 us -> 0 us
  other arithmetic: 10.8 us -> 0 us
    gather x22 -> x0, local copies, waits for them, and re-layouts: 121 us -> none  [the longest x14 95.8 us: pack_index(): jnp.searchsorted(column, targets, side='left')]
    all_to_all x1 -> x0, blocking collectives: 98.1 us -> none  [local_step(): recv_buf = lax.all_to_all(send_buf, 'ep', 1, 1, tiled=True)]
    all_to_all x1 -> x0, waiting for transfers between devices: 89.9 us -> none  [local_step(): lax.all_to_all(expert_out.reshape(local_n, group_n, capacity, d_model), '...]
    pallas_call x0 -> x3, Pallas kernels: none -> 73.8 us  [the longest x1 33.8 us: local_step(): pl.pallas_call(combine_kernel, out_shape=[on_chip(wd_on.shape, BF16), jax...]
    dot_general x2 -> x0, matrix products: 72.1 us -> none  [the longest x1 41.6 us: expert_ffn(): jnp.einsum('erf,efd->erd', hidden, wd_loc, preferred_element_type=jnp.flo...]
    all_to_all x2 -> x0, local copies, waits for them, and re-layouts: 16.6 us -> none  [the longest x1 8.33 us: local_step(): recv_buf = lax.all_to_all(send_buf, 'ep', 1, 1, tiled=True)]
    reshape x1 -> x0, local copies, waits for them, and re-layouts: 8.35 us -> none  [local_step(): expert_out.reshape(local_n, group_n, capacity, d_model)]
    reduce_sum x2 -> x0, other arithmetic: 5.77 us -> none  [the longest x1 4.93 us: combine_rows(): jnp.sum(gate_loc[:, :, None] * picked.astype(jnp.float32), axis=1)]
  transfers between devices with their start and end apart: 1 -> 0, of which waited for: 1 -> 0; matrix products, arithmetic and copies ran while one was open for 1% -> 0% of each run, Pallas kernels for 0% -> 0%
where the time goes in v1:
time: 74.8 us; the launch traced here: 74.6 us
  Pallas kernels  73.8 us (99%)
    pallas_call x1, Pallas kernels, local_step(): pl.pallas_call(combine_kernel, out_shape=[on_chip(wd_on.shape, BF16), jax...  33.8 us
    pallas_call x1, Pallas kernels, local_step(): pl.pallas_call(hidden_kernel, out_shape=[on_chip(w_on.shape, BF16), on_ch...  22.5 us
    pallas_call x1, Pallas kernels, local_step(): pl.pallas_call(gather_kernel, out_shape=[on_chip((SLOTS, 2, d_model, d_ff...  17.6 us

profile of v1, /device:TPU:0, one launch (start us, length us, event | category | flops | bytes accessed | tf_op | source)
XLA Modules:
  0.0 74.6 jit_solution(16976041800258660361)
XLA Ops:
  0.0 17.6 %gather.1 = (bf16[3,2,2048,1408]{3,2,1,0:T(8,128)(2,1)S(1)}, bf16[512,2048]{1,0:T(8,128)(2,1)S(1)}, f32[8,16,128]{2,1,0:T(8,128)S(1)}, bf16[8,256,1408]{2,1,0:T(...) custom-call(bf16[64,2048]{1,0:T(8,128)(2,1)} %tok.1, s32[6,64]{1,0:T(8,128)} %bitcast.2, ...), custom_call_target="tpu_custom_call" | custom-call | tf_op jit(solution)/shard_map/gather/pallas_call | solution.py:330
  17.6 22.5 %hidden.1 = (bf16[3,2,2048,1408]{3,2,1,0:T(8,128)(2,1)S(1)}, bf16[8,256,1408]{2,1,0:T(8,128)(2,1)S(1)}, bf16[4,3,128,256]{3,2,1,0:T(8,128)(2,1)S(1)}, bf16[2,8,1408,256]{3,2,1,0:T(8,128)(2,1)S(1)}) custom-call(bf16[3,2,2048,1408]{3,2,1,0:T(8,128)(2,1)S(1)} %get-tuple-element.15.w_in, ...), custom_call_target="tpu_custom_call", output_to_operand_aliasing={{0}: (0, {}), {1}: (1, {}), {2}: (2, {}), {3}: (3, {})} | custom-call | tf_op jit(solution)/shard_map/hidden/pallas_call | solution.py:339
  40.0 33.8 %combine.1 = (bf16[2,8,1408,256]{3,2,1,0:T(8,128)(2,1)S(1)}, bf16[64,2048]{1,0:T(8,128)(2,1)S(1)}) custom-call(bf16[2,8,1408,256]{3,2,1,0:T(8,128)(2,1)S(1)} %get-tuple-element.21.wd_in, bf16[8,256,1408]{2,1,0:T(8,128)(2,1)S(1)} %get-tuple-element.22.h, bf16[4,3,128,256]{3,2,1,0:T(8,128)(2,1)S(1)} %get-tuple-element.23.s, ...), custom_call_target="tpu_custom_call", output_to_operand_aliasing={{0}: (0, {})} | custom-call | tf_op jit(solution)/shard_map/combine/pallas_call | solution.py:349
  73.9 0.7 copy.18

commit v2 on v1

--- a/solution.py
+++ b/solution.py
@@ -10,7 +10,9 @@
 MESH = pl.DeviceIdType.MESH
 N_DEV = 8
 CAP = 32
-SLOTS = 3
+SLOTS = 4
+FRONT = 6
+LIMIT = 4 << 20
 COLS = 256
 VMEM = pl.BlockSpec(memory_space=pltpu.VMEM)
 ANY = pl.BlockSpec(memory_space=pl.ANY)
@@ -43,34 +45,43 @@
     pl.semaphore_wait(barrier, N_DEV - 1)
 
 
-def gather_kernel(tok, route_t, gate_t, wg, wu, w_out, x_out, sg_out, h_out, s_out, wd_out, pad, sg_loc, w_sem, sib_s, sib_r, link_s, link_r, sg_s, sg_r):
+def gather_kernel(tok, route_t, gate_t, wg, wu, wd, w_out, x_out, codes_out, h_out, s_out, wd_out, pad_i, pad_g, pad, sg_loc, sg, w_sem, d_sem, in_sem, sib_s, sib_r, link_s, link_r, sg_s, sg_r):
     me, core, x, y, sib, xn, yn = place()
+    n_tok = tok.shape[0]
+    half = n_tok // 2
+
+    def rows(device, part=0, count=half):
+        return x_out.at[pl.ds(pl.multiple_of(device * n_tok + part * half, half), count)]
+
+    own = pltpu.make_async_copy(tok, rows(me, 0, n_tok), in_sem.at[0])
+    own_route = pltpu.make_async_copy(route_t, pad_i, in_sem.at[1])
+    own_gate = pltpu.make_async_copy(gate_t, pad_g, in_sem.at[2])
+    own.start()
+    own_route.start()
+    own_gate.start()
     loads = []
     for e in range(SLOTS):
         loads.append(pltpu.make_async_copy(wg.at[e], w_out.at[e, 0], w_sem.at[e, 0]))
         loads.append(pltpu.make_async_copy(wu.at[e], w_out.at[e, 1], w_sem.at[e, 1]))
+    loads.append(pltpu.make_async_copy(wd.at[:, :, pl.ds(0, COLS)], wd_out, d_sem))
     for load in loads:
         load.start()
     entry_barrier(me)
 
-    n_tok = tok.shape[0]
-    half = n_tok // 2
-    first, second = pl.ds(0, half), pl.ds(half, half)
-
-    def rows(device, part=0, count=half):
-        return x_out.at[pl.ds(pl.multiple_of(device * n_tok + part * half, half), count)]
-
-    to_x_a = remote(tok.at[first], rows(me, 0), link_s.at[0], link_r.at[0], xn)
-    to_x_b = remote(tok.at[second], rows(me, 1), link_s.at[1], link_r.at[1], xn)
-    to_y_b = remote(tok.at[second], rows(me, 1), link_s.at[2], link_r.at[2], yn)
-    to_y_a = remote(tok.at[first], rows(me, 0), link_s.at[3], link_r.at[3], yn)
-    to_sib = remote(tok, rows(me, 0, n_tok), sib_s.at[0], sib_r.at[0], sib)
+    to_x_a = remote(rows(me, 0), rows(me, 0), link_s.at[0], link_r.at[0], xn)
+    to_x_b = remote(rows(me, 1), rows(me, 1), link_s.at[1], link_r.at[1], xn)
+    to_y_b = remote(rows(me, 1), rows(me, 1), link_s.at[2], link_r.at[2], yn)
+    to_y_a = remote(rows(me, 0), rows(me, 0), link_s.at[3], link_r.at[3], yn)
+    to_sib = remote(rows(me, 0, n_tok), rows(me, 0, n_tok), sib_s.at[0], sib_r.at[0], sib)
+    own.wait()
     for copy in (to_x_a, to_y_b, to_x_b, to_y_a, to_sib):
         copy.start()
 
     pad[...] = jnp.zeros_like(pad)
-    pad[0, 0:6, 0:n_tok] = route_t[...].astype(F32)
-    pad[1, 0:6, 0:n_tok] = gate_t[...]
+    own_route.wait()
+    pad[0, 0:6, 0:n_tok] = pad_i[...].astype(F32)
+    own_gate.wait()
+    pad[1, 0:6, 0:n_tok] = pad_g[...]
     routes = pad[0] + pltpu.roll(pad[0], n_tok, 1)
     gates = pad[1] + pltpu.roll(pad[1], n_tok, 1)
     expert = lax.broadcasted_iota(jnp.int32, (64, 128), 0).astype(F32)
@@ -89,14 +100,34 @@
     code = jnp.where(member > 0.5, rank + (me * CAP).astype(F32), 0.0)
     sg_loc[:, 0:8, :] = code.reshape(8, 8, 128)
     sg_loc[:, 8:16, :] = weight.reshape(8, 8, 128)
-    sg_out[me] = sg_loc[me]
+    sg[me] = sg_loc[me]
     sg_copies = []
     for d in range(1, N_DEV):
         peer = lax.rem(me + d, N_DEV)
-        sg_copies.append(remote(sg_loc.at[peer], sg_out.at[me], sg_s.at[d], sg_r.at[d], peer))
-    x_out[pl.ds(pl.multiple_of(me * n_tok, n_tok), n_tok), :] = tok[...]
+        sg_copies.append(remote(sg_loc.at[peer], sg.at[me], sg_s.at[d], sg_r.at[d], peer))
     for copy in sg_copies:
         copy.start()
+    for copy in sg_copies:
+        copy.wait()
+
+    r = lax.broadcasted_iota(jnp.int32, (256, 128), 0)
+    lane = lax.broadcasted_iota(jnp.int32, (256, 128), 1)
+    for p in range(4):
+        target = ((2 * p + lane // 64) * CAP + lax.rem(r, CAP) + 1).astype(F32)
+        code = sg[2 * p, 0:8, :] + sg[2 * p + 1, 0:8, :]
+        gate = sg[2 * p, 8:16, :] + sg[2 * p + 1, 8:16, :]
+        codes_out[:, pl.ds(p * 128, 128)] = code
+        code = jnp.broadcast_to(code[:, None, :], (8, CAP, 128)).reshape(256, 128)
+        gate = jnp.broadcast_to(gate[:, None, :], (8, CAP, 128)).reshape(256, 128)
+        s_t = jnp.where(code == target, gate, 0.0)
+        s_f = s_t.T
+        hi = jnp.minimum(s_f, 3.3895e38).astype(BF16)
+        rest = s_f - hi.astype(F32)
+        mid = rest.astype(BF16)
+        low = (rest - mid.astype(F32)).astype(BF16)
+        s_out[p, 0] = hi
+        s_out[p, 1] = mid
+        s_out[p, 2] = low
 
     dg = lax.rem(xn + 4, N_DEV)
     passed = []
@@ -125,19 +156,15 @@
     for copy in (to_x_a, to_x_b, to_y_b, to_y_a, via_y, via_x):
         copy.wait_send()
     to_sib.wait()
-    for copy in passed + sg_copies:
+    for copy in passed:
         copy.wait()
     for load in loads:
         load.wait()
 
 
-def hidden_kernel(w_in, h_in, s_in, wd_in, x_all, sg, wg, wu, wd, w_buf, h_out, s_out, wd_out, codes, xe, w_sem, d_sem):
+def hidden_kernel(w_in, h_in, x_all, codes, wg, wu, w_buf, h_out, xe, w_sem):
     n_exp = wg.shape[0]
     d_ff = wg.shape[2]
-    down = pltpu.make_async_copy(wd.at[:, :, pl.ds(0, COLS)], wd_out.at[0], d_sem)
-    down.start()
-    for p in range(4):
-        codes[:, pl.ds(p * 128, 128)] = sg[2 * p, 0:8, :] + sg[2 * p + 1, 0:8, :]
 
     def load(e, part, src):
         s = lax.rem(e, SLOTS)
@@ -203,37 +230,21 @@
 
     lax.fori_loop(0, n_exp, step, 0)
 
-    r = lax.broadcasted_iota(jnp.int32, (256, 128), 0)
-    lane = lax.broadcasted_iota(jnp.int32, (256, 128), 1)
-    for p in range(4):
-        target = ((2 * p + lane // 64) * CAP + lax.rem(r, CAP) + 1).astype(F32)
-        code = sg[2 * p, 0:8, :] + sg[2 * p + 1, 0:8, :]
-        gate = sg[2 * p, 8:16, :] + sg[2 * p + 1, 8:16, :]
-        code = jnp.broadcast_to(code[:, None, :], (8, CAP, 128)).reshape(256, 128)
-        gate = jnp.broadcast_to(gate[:, None, :], (8, CAP, 128)).reshape(256, 128)
-        s_t = jnp.where(code == target, gate, 0.0)
-        s_f = s_t.T
-        hi = jnp.minimum(s_f, 3.3895e38).astype(BF16)
-        rest = s_f - hi.astype(F32)
-        mid = rest.astype(BF16)
-        low = (rest - mid.astype(F32)).astype(BF16)
-        s_out[p, 0] = hi
-        s_out[p, 1] = mid
-        s_out[p, 2] = low
-    down.wait()
-
-
-def combine_kernel(wd_in, h, s, wd, wd_buf, y_out, o, part, d2d, h1a, h1b, h2a, h2b, w_sem, ds, dr, h1as, h1ar, h1bs, h1br, h2as, h2ar, h2bs, h2br):
+
+def combine_kernel(h, s, wd_on, wd, y_out, wd_buf, o, part, d2d, h1a, h1b, h2a, h2b, w_sem, ds, dr, h1as, h1ar, h1bs, h1br, h2as, h2ar, h2bs, h2br):
     me, core, x, y, sib, xn, yn = place()
     n_blk = wd.shape[2] // COLS
+    n_buf = wd_buf.shape[0]
+    n_exp = h.shape[0]
     half = 32
     first, second = pl.ds(0, half), pl.ds(half, half)
 
     def load(b):
-        s_ = lax.rem(b, 2)
-        return pltpu.make_async_copy(wd.at[:, :, pl.ds(pl.multiple_of(b * COLS, COLS), COLS)], wd_buf.at[s_], w_sem.at[s_])
-
-    load(1).start()
+        slot = lax.rem(b - 1, n_buf)
+        return pltpu.make_async_copy(wd.at[:, :, pl.ds(pl.multiple_of(b * COLS, COLS), COLS)], wd_buf.at[slot], w_sem.at[slot])
+
+    for b in range(1, n_buf + 1):
+        load(b).start()
     entry_barrier(me)
 
     def send_d2d(b):
@@ -280,35 +291,53 @@
         y_out[first, cols] = (part[b, core, y, x, first] + h2a[b]).astype(BF16)
         y_out[second, cols] = (part[b, core, y, x, second] + h2b[b]).astype(BF16)
 
-    def compute(b):
-        slot = lax.rem(b, 2)
-
-        @pl.when((b >= 1) & (b + 1 < n_blk))
-        def _():
-            load(b + 1).start()
-
-        @pl.when(b >= 1)
-        def _():
-            load(b).wait()
-
-        for e in range(h.shape[0]):
-            out = jnp.dot(h[e], wd_buf[slot, e], preferred_element_type=F32).astype(BF16)
-            for i in range(N_DEV):
-                o[i, pl.ds(e * CAP, CAP), :] = out[i * CAP : (i + 1) * CAP]
+    def down(e, weights):
+        out = jnp.dot(h[e], weights[e], preferred_element_type=F32).astype(BF16)
         for i in range(N_DEV):
-            gates = s[i // 2, :, pl.ds((i % 2) * 64, 64), :].reshape(192, 256)
-            terms = jnp.dot(gates, o[i], preferred_element_type=F32)
-            part[b, i % 2, i // 4, (i // 2) % 2] = terms[0:64] + terms[64:128] + terms[128:192]
+            o[i, pl.ds(e * CAP, CAP), :] = out[i * CAP : (i + 1) * CAP]
+
+    def on_weights(b, body):
+        @pl.when(b == 0)
+        def _():
+            body(wd_on)
+
+        @pl.when((b >= 1) & (b < n_blk))
+        def _():
+            body(wd_buf.at[lax.rem(b - 1, n_buf)])
 
     def step(b, carry):
         lag(b, 1, stage_1)
-        lag(b, 2, stage_2)
+
+        @pl.when((b >= 1) & (b < n_blk))
+        def _():
+            load(b).wait()
+
+        def front(weights):
+            for e in range(FRONT):
+                down(e, weights)
+
+        on_weights(b, front)
+        lag(b, 1, stage_2)
         lag(b, 3, stage_3)
-        lag(b, 4, stage_4)
-        lag(b, 0, compute)
+        lag(b, 5, stage_4)
+
+        def back(weights):
+            for e in range(FRONT, n_exp):
+                down(e, weights)
+            for i in range(N_DEV):
+                gates = s[i // 2, :, pl.ds((i % 2) * 64, 64), :].reshape(192, 256)
+                terms = jnp.dot(gates, o[i], preferred_element_type=F32)
+                part[b, i % 2, i // 4, (i // 2) % 2] = terms[0:64] + terms[64:128] + terms[128:192]
+
+        on_weights(b, back)
+
+        @pl.when((b >= 1) & (b + n_buf < n_blk))
+        def _():
+            load(b + n_buf).start()
+
         return carry
 
-    lax.fori_loop(0, n_blk + 4, step, 0)
+    lax.fori_loop(0, n_blk + 5, step, 0)
 
     def drain(b, carry):
         for send in (send_d2d, send_1a, send_1b, send_2a, send_2b):
@@ -327,31 +356,48 @@
         n_exp, d_model, d_ff = wg.shape
         n_tok = tok.shape[0]
         n_blk = d_model // COLS
-        w_on, x_all, sg, h, s, wd_on = pl.pallas_call(
+        hidden = (n_exp, N_DEV * CAP, d_ff)
+        w_on, x_all, codes, h, s, wd_on = pl.pallas_call(
             gather_kernel,
-            out_shape=[on_chip((SLOTS, 2, d_model, d_ff), BF16), on_chip((N_DEV * n_tok, d_model), BF16), on_chip((N_DEV, 16, 128), F32), on_chip((n_exp, N_DEV * CAP, d_ff), BF16), on_chip((4, 3, 128, 256), BF16), on_chip((2, n_exp, d_ff, COLS), BF16)],
-            in_specs=[VMEM, VMEM, VMEM, ANY, ANY],
+            out_shape=[on_chip((SLOTS, 2, d_model, d_ff), BF16), on_chip((N_DEV * n_tok, d_model), BF16), on_chip((8, 512), F32), on_chip(hidden, BF16), on_chip((4, 3, 128, 256), BF16), on_chip((n_exp, d_ff, COLS), BF16)],
+            in_specs=[ANY] * 6,
             out_specs=[VMEM] * 6,
-            scratch_shapes=[pltpu.VMEM((2, 8, 128), F32), pltpu.VMEM((N_DEV, 16, 128), F32), dma((SLOTS, 2)), dma((7,)), dma((7,)), dma((6,)), dma((6,)), dma((N_DEV,)), dma((N_DEV,))],
-            compiler_params=pltpu.CompilerParams(collective_id=0, has_side_effects=True, vmem_limit_bytes=6 << 20),
+            scratch_shapes=[
+                pltpu.VMEM((6, n_tok), jnp.int32),
+                pltpu.VMEM((6, n_tok), F32),
+                pltpu.VMEM((2, 8, 128), F32),
+                pltpu.VMEM((N_DEV, 16, 128), F32),
+                pltpu.VMEM((N_DEV, 16, 128), F32),
+                dma((SLOTS, 2)),
+                dma,
+                dma((3,)),
+                dma((7,)),
+                dma((7,)),
+                dma((6,)),
+                dma((6,)),
+                dma((N_DEV,)),
+                dma((N_DEV,)),
+            ],
+            compiler_params=pltpu.CompilerParams(collective_id=0, has_side_effects=True, vmem_limit_bytes=LIMIT),
             name="gather",
-        )(tok, route.T, gate.T, wg, wu)
-        unused, h, s, wd_on = pl.pallas_call(
+        )(tok, route.T, gate.T, wg, wu, wd)
+        unused, h = pl.pallas_call(
             hidden_kernel,
-            out_shape=[on_chip(w_on.shape, BF16), on_chip((n_exp, N_DEV * CAP, d_ff), BF16), on_chip((4, 3, 128, 256), BF16), on_chip((2, n_exp, d_ff, COLS), BF16)],
-            in_specs=[VMEM] * 6 + [ANY] * 3,
-            out_specs=[VMEM] * 4,
-            scratch_shapes=[pltpu.VMEM((8, 512), F32), pltpu.VMEM((256, d_model), BF16), dma((SLOTS, 2)), dma],
-            input_output_aliases={0: 0, 1: 1, 2: 2, 3: 3},
-            compiler_params=pltpu.CompilerParams(vmem_limit_bytes=6 << 20),
+            out_shape=[on_chip(w_on.shape, BF16), on_chip(hidden, BF16)],
+            in_specs=[VMEM] * 4 + [ANY] * 2,
+            out_specs=[VMEM] * 2,
+            scratch_shapes=[pltpu.VMEM((256, d_model), BF16), dma((SLOTS, 2))],
+            input_output_aliases={0: 0, 1: 1},
+            compiler_params=pltpu.CompilerParams(vmem_limit_bytes=LIMIT),
             name="hidden",
-        )(pin(w_on), pin(h), pin(s), pin(wd_on), pin(x_all), pin(sg), wg, wu, wd)
-        out = pl.pallas_call(
+        )(pin(w_on), pin(h), pin(x_all), pin(codes), wg, wu)
+        return pl.pallas_call(
             combine_kernel,
-            out_shape=[on_chip(wd_on.shape, BF16), jax.ShapeDtypeStruct((n_tok, d_model), BF16)],
-            in_specs=[VMEM, VMEM, VMEM, ANY],
-            out_specs=[VMEM] * 2,
+            out_shape=jax.ShapeDtypeStruct((n_tok, d_model), BF16),
+            in_specs=[VMEM] * 3 + [ANY],
+            out_specs=VMEM,
             scratch_shapes=[
+                pltpu.VMEM((3, n_exp, d_ff, COLS), BF16),
                 pltpu.VMEM((N_DEV, 256, COLS), BF16),
                 pltpu.VMEM((n_blk, 2, 2, 2, n_tok, COLS), F32),
                 pltpu.VMEM((n_blk, 2, 2, n_tok, COLS), F32),
@@ -359,13 +405,11 @@
                 pltpu.VMEM((n_blk, 2, n_tok // 2, COLS), F32),
                 pltpu.VMEM((n_blk, n_tok // 2, COLS), F32),
                 pltpu.VMEM((n_blk, n_tok // 2, COLS), F32),
-                dma((2,)),
+                dma((3,)),
             ]
             + [dma((n_blk,))] * 10,
-            input_output_aliases={0: 0},
-            compiler_params=pltpu.CompilerParams(collective_id=1, has_side_effects=True, vmem_limit_bytes=16 << 20),
+            compiler_params=pltpu.CompilerParams(collective_id=1, has_side_effects=True, vmem_limit_bytes=32 << 20),
             name="combine",
-        )(pin(wd_on), pin(h), pin(s), wd)
-        return out[1]
+        )(pin(h), pin(s), pin(wd_on), wd)
 
     return jax.shard_map(local_step, mesh=mesh, in_specs=(row_spec, row_spec, row_spec, expert_spec, expert_spec, expert_spec), out_specs=row_spec, check_vma=False)

time: 74.8 us -> 80 us (1.070)
  Pallas kernels: 73.8 us -> 79.2 us
    pallas_call x1, Pallas kernels: 17.6 us -> 28.5 us  [local_step(): pl.pallas_call(gather_kernel, out_shape=[on_chip((SLOTS, 2, d_model, d_ff...]
    pallas_call x1, Pallas kernels: 22.5 us -> 19 us  [local_step(): pl.pallas_call(hidden_kernel, out_shape=[on_chip(w_on.shape, BF16), on_ch...]
    pallas_call x1, Pallas kernels: 33.8 us -> 31.7 us  [local_step(): pl.pallas_call(combine_kernel, out_shape=jax.ShapeDtypeStruct((n_tok, d_m...]
where the time goes in v2:
time: 80 us; the launch traced here: 79.9 us
  Pallas kernels  79.2 us (99%)
    pallas_call x1, Pallas kernels, local_step(): pl.pallas_call(combine_kernel, out_shape=jax.ShapeDtypeStruct((n_tok, d_m...  31.7 us
    pallas_call x1, Pallas kernels, local_step(): pl.pallas_call(gather_kernel, out_shape=[on_chip((SLOTS, 2, d_model, d_ff...  28.5 us
    pallas_call x1, Pallas kernels, local_step(): pl.pallas_call(hidden_kernel, out_shape=[on_chip(w_on.shape, BF16), on_ch...  19 us

profile of v2, /device:TPU:0, one launch (start us, length us, event | category | flops | bytes accessed | tf_op | source)
XLA Modules:
  0.0 79.9 jit_solution(16485256302108355699)
XLA Ops:
  0.0 28.5 %gather.1 = (bf16[4,2,2048,1408]{3,2,1,0:T(8,128)(2,1)S(1)}, bf16[512,2048]{1,0:T(8,128)(2,1)S(1)}, f32[8,512]{1,0:T(8,128)S(1)}, bf16[8,256,1408]{2,1,0:T(8,128...) custom-call(bf16[64,2048]{1,0:T(8,128)(2,1)} %tok.1, s32[6,64]{1,0:T(8,128)} %bitcast.2, ...), custom_call_target="tpu_custom_call" | custom-call | tf_op jit(solution)/shard_map/gather/pallas_call | solution.py:360
  28.5 19.0 %hidden.1 = (bf16[4,2,2048,1408]{3,2,1,0:T(8,128)(2,1)S(1)}, bf16[8,256,1408]{2,1,0:T(8,128)(2,1)S(1)}) custom-call(bf16[4,2,2048,1408]{3,2,1,0:T(8,128)(2,1)S(1)} %get-tuple-element.12.w_in, bf16[8,256,1408]{2,1,0:T(8,128)(2,1)S(1)} %get-tuple-element.13.h_in, ...), custom_call_target="tpu_custom_call", output_to_operand_aliasing={{0}: (0, {}), {1}: (1, {})} | custom-call | tf_op jit(solution)/shard_map/hidden/pallas_call | solution.py:384
  47.4 31.7 %combine.1 = bf16[64,2048]{1,0:T(8,128)(2,1)S(1)} custom-call(bf16[8,256,1408]{2,1,0:T(8,128)(2,1)S(1)} %get-tuple-element.16.h, bf16[4,3,128,256]{3,2,1,0:T(8,128)(2,1)S(1)} %get-tuple-element.17.s, bf16[8,1408,256]{2,1,0:T(8,128)(2,1)S(1)} %get-tuple-element.18.wd_on, bf16[8,1408,2048]{2,1,0:T(8,128)(2,1)} %wd.3), custom_call_target="tpu_custom_call" | custom-call | tf_op jit(solution)/shard_map/combine/pallas_call | solution.py:394
  79.2 0.7 copy.12

commit v3 on v2

--- a/solution.py
+++ b/solution.py
@@ -64,10 +64,14 @@
         loads.append(pltpu.make_async_copy(wg.at[e], w_out.at[e, 0], w_sem.at[e, 0]))
         loads.append(pltpu.make_async_copy(wu.at[e], w_out.at[e, 1], w_sem.at[e, 1]))
     loads.append(pltpu.make_async_copy(wd.at[:, :, pl.ds(0, COLS)], wd_out, d_sem))
-    for load in loads:
-        load.start()
     entry_barrier(me)
 
+    def bring(count):
+        for load in loads[bring.done : bring.done + count]:
+            load.start()
+        bring.done += count
+
+    bring.done = 0
     to_x_a = remote(rows(me, 0), rows(me, 0), link_s.at[0], link_r.at[0], xn)
     to_x_b = remote(rows(me, 1), rows(me, 1), link_s.at[1], link_r.at[1], xn)
     to_y_b = remote(rows(me, 1), rows(me, 1), link_s.at[2], link_r.at[2], yn)
@@ -76,6 +80,7 @@
     own.wait()
     for copy in (to_x_a, to_y_b, to_x_b, to_y_a, to_sib):
         copy.start()
+    bring(4)
 
     pad[...] = jnp.zeros_like(pad)
     own_route.wait()
@@ -141,18 +146,23 @@
     via_y = remote(rows(xn, 0), rows(xn, 0), link_s.at[4], link_r.at[4], yn)
     via_y.start()
     pass_on(1, xn, 0)
+    bring(1)
     to_y_b.wait_recv()
     via_x = remote(rows(yn, 1), rows(yn, 1), link_s.at[5], link_r.at[5], xn)
     via_x.start()
     pass_on(2, yn, 1)
+    bring(1)
     to_x_b.wait_recv()
     pass_on(3, xn, 1)
+    bring(1)
     to_y_a.wait_recv()
     pass_on(4, yn, 0)
+    bring(1)
     via_y.wait_recv()
     pass_on(5, dg, 0)
     via_x.wait_recv()
     pass_on(6, dg, 1)
+    bring(1)
     for copy in (to_x_a, to_x_b, to_y_b, to_y_a, via_y, via_x):
         copy.wait_send()
     to_sib.wait()

time: 80 us -> 74.9 us (0.936)
  Pallas kernels: 79.2 us -> 73.6 us
    pallas_call x1, Pallas kernels: 28.5 us -> 22.3 us  [local_step(): pl.pallas_call(gather_kernel, out_shape=[on_chip((SLOTS, 2, d_model, d_ff...]
    pallas_call x1, Pallas kernels: 19 us -> 19.8 us  [local_step(): pl.pallas_call(hidden_kernel, out_shape=[on_chip(w_on.shape, BF16), on_ch...]
where the time goes in v3:
time: 74.9 us; the launch traced here: 74.3 us
  Pallas kernels  73.6 us (98%)
    pallas_call x1, Pallas kernels, local_step(): pl.pallas_call(combine_kernel, out_shape=jax.ShapeDtypeStruct((n_tok, d_m...  31.5 us
    pallas_call x1, Pallas kernels, local_step(): pl.pallas_call(gather_kernel, out_shape=[on_chip((SLOTS, 2, d_model, d_ff...  22.3 us
    pallas_call x1, Pallas kernels, local_step(): pl.pallas_call(hidden_kernel, out_shape=[on_chip(w_on.shape, BF16), on_ch...  19.8 us

profile of v3, /device:TPU:0, one launch (start us, length us, event | category | flops | bytes accessed | tf_op | source)
XLA Modules:
  0.0 74.3 jit_solution(5726903829361069575)
XLA Ops:
  0.0 22.3 %gather.1 = (bf16[4,2,2048,1408]{3,2,1,0:T(8,128)(2,1)S(1)}, bf16[512,2048]{1,0:T(8,128)(2,1)S(1)}, f32[8,512]{1,0:T(8,128)S(1)}, bf16[8,256,1408]{2,1,0:T(8,128...) custom-call(bf16[64,2048]{1,0:T(8,128)(2,1)} %tok.1, s32[6,64]{1,0:T(8,128)} %bitcast.2, ...), custom_call_target="tpu_custom_call" | custom-call | tf_op jit(solution)/shard_map/gather/pallas_call | solution.py:370
  22.3 19.8 %hidden.1 = (bf16[4,2,2048,1408]{3,2,1,0:T(8,128)(2,1)S(1)}, bf16[8,256,1408]{2,1,0:T(8,128)(2,1)S(1)}) custom-call(bf16[4,2,2048,1408]{3,2,1,0:T(8,128)(2,1)S(1)} %get-tuple-element.12.w_in, bf16[8,256,1408]{2,1,0:T(8,128)(2,1)S(1)} %get-tuple-element.13.h_in, ...), custom_call_target="tpu_custom_call", output_to_operand_aliasing={{0}: (0, {}), {1}: (1, {})} | custom-call | tf_op jit(solution)/shard_map/hidden/pallas_call | solution.py:394
  42.1 31.5 %combine.1 = bf16[64,2048]{1,0:T(8,128)(2,1)S(1)} custom-call(bf16[8,256,1408]{2,1,0:T(8,128)(2,1)S(1)} %get-tuple-element.16.h, bf16[4,3,128,256]{3,2,1,0:T(8,128)(2,1)S(1)} %get-tuple-element.17.s, bf16[8,1408,256]{2,1,0:T(8,128)(2,1)S(1)} %get-tuple-element.18.wd_on, bf16[8,1408,2048]{2,1,0:T(8,128)(2,1)} %wd.3), custom_call_target="tpu_custom_call" | custom-call | tf_op jit(solution)/shard_map/combine/pallas_call | solution.py:404
  73.6 0.7 copy.12

commit v4 on v2

--- a/solution.py
+++ b/solution.py
@@ -11,6 +11,7 @@
 N_DEV = 8
 CAP = 32
 SLOTS = 4
+EARLY = 3
 FRONT = 6
 LIMIT = 4 << 20
 COLS = 256
@@ -45,7 +46,7 @@
     pl.semaphore_wait(barrier, N_DEV - 1)
 
 
-def gather_kernel(tok, route_t, gate_t, wg, wu, wd, w_out, x_out, codes_out, h_out, s_out, wd_out, pad_i, pad_g, pad, sg_loc, sg, w_sem, d_sem, in_sem, sib_s, sib_r, link_s, link_r, sg_s, sg_r):
+def gather_kernel(tok, route_t, gate_t, wg, wu, w_out, x_out, codes_out, h_out, s_out, wd_out, pad_i, pad_g, pad, sg_loc, sg, w_sem, in_sem, sib_s, sib_r, link_s, link_r, sg_s, sg_r):
     me, core, x, y, sib, xn, yn = place()
     n_tok = tok.shape[0]
     half = n_tok // 2
@@ -59,23 +60,15 @@
     own.start()
     own_route.start()
     own_gate.start()
+    barrier = pltpu.get_barrier_semaphore()
+    for d in range(1, N_DEV):
+        pl.semaphore_signal(barrier, inc=1, device_id={"ep": lax.rem(me + d, N_DEV)}, device_id_type=MESH)
     loads = []
-    for e in range(SLOTS):
+    for e in range(EARLY):
         loads.append(pltpu.make_async_copy(wg.at[e], w_out.at[e, 0], w_sem.at[e, 0]))
         loads.append(pltpu.make_async_copy(wu.at[e], w_out.at[e, 1], w_sem.at[e, 1]))
-    loads.append(pltpu.make_async_copy(wd.at[:, :, pl.ds(0, COLS)], wd_out, d_sem))
     for load in loads:
         load.start()
-    entry_barrier(me)
-
-    to_x_a = remote(rows(me, 0), rows(me, 0), link_s.at[0], link_r.at[0], xn)
-    to_x_b = remote(rows(me, 1), rows(me, 1), link_s.at[1], link_r.at[1], xn)
-    to_y_b = remote(rows(me, 1), rows(me, 1), link_s.at[2], link_r.at[2], yn)
-    to_y_a = remote(rows(me, 0), rows(me, 0), link_s.at[3], link_r.at[3], yn)
-    to_sib = remote(rows(me, 0, n_tok), rows(me, 0, n_tok), sib_s.at[0], sib_r.at[0], sib)
-    own.wait()
-    for copy in (to_x_a, to_y_b, to_x_b, to_y_a, to_sib):
-        copy.start()
 
     pad[...] = jnp.zeros_like(pad)
     own_route.wait()
@@ -101,12 +94,38 @@
     sg_loc[:, 0:8, :] = code.reshape(8, 8, 128)
     sg_loc[:, 8:16, :] = weight.reshape(8, 8, 128)
     sg[me] = sg_loc[me]
+    pl.semaphore_wait(barrier, N_DEV - 1)
+
     sg_copies = []
     for d in range(1, N_DEV):
         peer = lax.rem(me + d, N_DEV)
         sg_copies.append(remote(sg_loc.at[peer], sg.at[me], sg_s.at[d], sg_r.at[d], peer))
     for copy in sg_copies:
         copy.start()
+    to_x_a = remote(rows(me, 0), rows(me, 0), link_s.at[0], link_r.at[0], xn)
+    to_x_b = remote(rows(me, 1), rows(me, 1), link_s.at[1], link_r.at[1], xn)
+    to_y_b = remote(rows(me, 1), rows(me, 1), link_s.at[2], link_r.at[2], yn)
+    to_y_a = remote(rows(me, 0), rows(me, 0), link_s.at[3], link_r.at[3], yn)
+    to_sib = remote(rows(me, 0, n_tok), rows(me, 0, n_tok), sib_s.at[0], sib_r.at[0], sib)
+    own.wait()
+    for copy in (to_x_a, to_y_b, to_x_b, to_y_a, to_sib):
+        copy.start()
+    dg = lax.rem(xn + 4, N_DEV)
+    passed = []
+
+    def pass_on(index, source, part):
+        copy = remote(rows(source, part), rows(source, part), sib_s.at[index], sib_r.at[index], sib)
+        copy.start()
+        passed.append(copy)
+
+    to_x_a.wait_recv()
+    via_y = remote(rows(xn, 0), rows(xn, 0), link_s.at[4], link_r.at[4], yn)
+    via_y.start()
+    pass_on(1, xn, 0)
+    to_y_b.wait_recv()
+    via_x = remote(rows(yn, 1), rows(yn, 1), link_s.at[5], link_r.at[5], xn)
+    via_x.start()
+    pass_on(2, yn, 1)
     for copy in sg_copies:
         copy.wait()
 
@@ -129,22 +148,6 @@
         s_out[p, 1] = mid
         s_out[p, 2] = low
 
-    dg = lax.rem(xn + 4, N_DEV)
-    passed = []
-
-    def pass_on(index, source, part):
-        copy = remote(rows(source, part), rows(source, part), sib_s.at[index], sib_r.at[index], sib)
-        copy.start()
-        passed.append(copy)
-
-    to_x_a.wait_recv()
-    via_y = remote(rows(xn, 0), rows(xn, 0), link_s.at[4], link_r.at[4], yn)
-    via_y.start()
-    pass_on(1, xn, 0)
-    to_y_b.wait_recv()
-    via_x = remote(rows(yn, 1), rows(yn, 1), link_s.at[5], link_r.at[5], xn)
-    via_x.start()
-    pass_on(2, yn, 1)
     to_x_b.wait_recv()
     pass_on(3, xn, 1)
     to_y_a.wait_recv()
@@ -162,13 +165,18 @@
         load.wait()
 
 
-def hidden_kernel(w_in, h_in, x_all, codes, wg, wu, w_buf, h_out, xe, w_sem):
+def hidden_kernel(w_in, h_in, wd_in, x_all, codes, wg, wu, wd, w_buf, h_out, wd_out, xe, w_sem, d_sem):
     n_exp = wg.shape[0]
     d_ff = wg.shape[2]
 
     def load(e, part, src):
         s = lax.rem(e, SLOTS)
         return pltpu.make_async_copy(src.at[e], w_buf.at[s, part], w_sem.at[s, part])
+
+    for e in range(EARLY, SLOTS):
+        load(e, 0, wg).start()
+        load(e, 1, wu).start()
+    down = pltpu.make_async_copy(wd.at[:, :, pl.ds(0, COLS)], wd_out, d_sem)
 
     def hidden_rows(e, cap, slot):
         m = cap * N_DEV
@@ -203,7 +211,7 @@
     def step(e, carry):
         slot = lax.rem(e, SLOTS)
 
-        @pl.when(e >= SLOTS)
+        @pl.when(e >= EARLY)
         def _():
             load(e, 0, wg).wait()
             load(e, 1, wu).wait()
@@ -226,9 +234,14 @@
             load(e + SLOTS, 0, wg).start()
             load(e + SLOTS, 1, wu).start()
 
+        @pl.when(e + SLOTS == n_exp)
+        def _():
+            down.start()
+
         return carry
 
     lax.fori_loop(0, n_exp, step, 0)
+    down.wait()
 
 
 def combine_kernel(h, s, wd_on, wd, y_out, wd_buf, o, part, d2d, h1a, h1b, h2a, h2b, w_sem, ds, dr, h1as, h1ar, h1bs, h1br, h2as, h2ar, h2bs, h2br):
@@ -360,7 +373,7 @@
         w_on, x_all, codes, h, s, wd_on = pl.pallas_call(
             gather_kernel,
             out_shape=[on_chip((SLOTS, 2, d_model, d_ff), BF16), on_chip((N_DEV * n_tok, d_model), BF16), on_chip((8, 512), F32), on_chip(hidden, BF16), on_chip((4, 3, 128, 256), BF16), on_chip((n_exp, d_ff, COLS), BF16)],
-            in_specs=[ANY] * 6,
+            in_specs=[ANY] * 5,
             out_specs=[VMEM] * 6,
             scratch_shapes=[
                 pltpu.VMEM((6, n_tok), jnp.int32),
@@ -368,8 +381,7 @@
                 pltpu.VMEM((2, 8, 128), F32),
                 pltpu.VMEM((N_DEV, 16, 128), F32),
                 pltpu.VMEM((N_DEV, 16, 128), F32),
-                dma((SLOTS, 2)),
-                dma,
+                dma((EARLY, 2)),
                 dma((3,)),
                 dma((7,)),
                 dma((7,)),
@@ -380,17 +392,17 @@
             ],
             compiler_params=pltpu.CompilerParams(collective_id=0, has_side_effects=True, vmem_limit_bytes=LIMIT),
             name="gather",
-        )(tok, route.T, gate.T, wg, wu, wd)
-        unused, h = pl.pallas_call(
+        )(tok, route.T, gate.T, wg, wu)
+        unused, h, wd_on = pl.pallas_call(
             hidden_kernel,
-            out_shape=[on_chip(w_on.shape, BF16), on_chip(hidden, BF16)],
-            in_specs=[VMEM] * 4 + [ANY] * 2,
-            out_specs=[VMEM] * 2,
-            scratch_shapes=[pltpu.VMEM((256, d_model), BF16), dma((SLOTS, 2))],
-            input_output_aliases={0: 0, 1: 1},
+            out_shape=[on_chip(w_on.shape, BF16), on_chip(hidden, BF16), on_chip(wd_on.shape, BF16)],
+            in_specs=[VMEM] * 5 + [ANY] * 3,
+            out_specs=[VMEM] * 3,
+            scratch_shapes=[pltpu.VMEM((256, d_model), BF16), dma((SLOTS, 2)), dma],
+            input_output_aliases={0: 0, 1: 1, 2: 2},
             compiler_params=pltpu.CompilerParams(vmem_limit_bytes=LIMIT),
             name="hidden",
-        )(pin(w_on), pin(h), pin(x_all), pin(codes), wg, wu)
+        )(pin(w_on), pin(h), pin(wd_on), pin(x_all), pin(codes), wg, wu, wd)
         return pl.pallas_call(
             combine_kernel,
             out_shape=jax.ShapeDtypeStruct((n_tok, d_model), BF16),

time: 80 us -> 68.3 us (0.85)
  Pallas kernels: 79.2 us -> 67.4 us
    pallas_call x1, Pallas kernels: 28.5 us -> 16.6 us  [local_step(): pl.pallas_call(gather_kernel, out_shape=[on_chip((SLOTS, 2, d_model, d_ff...]
    pallas_call x1, Pallas kernels: 19 us -> 21.6 us  [local_step(): pl.pallas_call(hidden_kernel, out_shape=[on_chip(w_on.shape, BF16), on_ch...]
    pallas_call x1, Pallas kernels: 31.7 us -> 29.2 us  [local_step(): pl.pallas_call(combine_kernel, out_shape=jax.ShapeDtypeStruct((n_tok, d_m...]
where the time goes in v4:
time: 68.3 us; the launch traced here: 68.1 us
  Pallas kernels  67.4 us (99%)
  local copies, waits for them, and re-layouts  0.71 us (1%)
    pallas_call x1, Pallas kernels, local_step(): pl.pallas_call(combine_kernel, out_shape=jax.ShapeDtypeStruct((n_tok, d_m...  29.2 us
    pallas_call x1, Pallas kernels, local_step(): pl.pallas_call(hidden_kernel, out_shape=[on_chip(w_on.shape, BF16), on_ch...  21.6 us
    pallas_call x1, Pallas kernels, local_step(): pl.pallas_call(gather_kernel, out_shape=[on_chip((SLOTS, 2, d_model, d_ff...  16.6 us

profile of v4, /device:TPU:0, one launch (start us, length us, event | category | flops | bytes accessed | tf_op | source)
XLA Modules:
  0.0 68.1 jit_solution(1810492656372103612)
XLA Ops:
  0.0 16.6 %gather.1 = (bf16[4,2,2048,1408]{3,2,1,0:T(8,128)(2,1)S(1)}, bf16[512,2048]{1,0:T(8,128)(2,1)S(1)}, f32[8,512]{1,0:T(8,128)S(1)}, bf16[8,256,1408]{2,1,0:T(8,128...) custom-call(bf16[64,2048]{1,0:T(8,128)(2,1)} %tok.1, s32[6,64]{1,0:T(8,128)} %bitcast.2, ...), custom_call_target="tpu_custom_call" | custom-call | tf_op jit(solution)/shard_map/gather/pallas_call | solution.py:373
  16.6 21.6 %hidden.1 = (bf16[4,2,2048,1408]{3,2,1,0:T(8,128)(2,1)S(1)}, bf16[8,256,1408]{2,1,0:T(8,128)(2,1)S(1)}, bf16[8,1408,256]{2,1,0:T(8,128)(2,1)S(1)}) custom-call(bf16[4,2,2048,1408]{3,2,1,0:T(8,128)(2,1)S(1)} %get-tuple-element.13.w_in, bf16[8,256,1408]{2,1,0:T(8,128)(2,1)S(1)} %get-tuple-element.14.h_in, ...), custom_call_target="tpu_custom_call", output_to_operand_aliasing={{0}: (0, {}), {1}: (1, {}), {2}: (2, {})} | custom-call | tf_op jit(solution)/shard_map/hidden/pallas_call | solution.py:396
  38.2 29.2 %combine.1 = bf16[64,2048]{1,0:T(8,128)(2,1)S(1)} custom-call(bf16[8,256,1408]{2,1,0:T(8,128)(2,1)S(1)} %get-tuple-element.18.h, bf16[4,3,128,256]{3,2,1,0:T(8,128)(2,1)S(1)} %get-tuple-element.19.s, bf16[8,1408,256]{2,1,0:T(8,128)(2,1)S(1)} %get-tuple-element.20.wd_on, bf16[8,1408,2048]{2,1,0:T(8,128)(2,1)} %wd.3), custom_call_target="tpu_custom_call" | custom-call | tf_op jit(solution)/shard_map/combine/pallas_call | solution.py:406
  67.4 0.7 %copy.14 = bf16[64,2048]{1,0:T(8,128)(2,1)} copy(bf16[64,2048]{1,0:T(8,128)(2,1)S(1)} %combine.1) | data formatting | bytes 524288

commit v5 on v4

--- a/solution.py
+++ b/solution.py
@@ -13,6 +13,8 @@
 SLOTS = 4
 EARLY = 3
 FRONT = 6
+LAG_3 = 3
+LAG_4 = 6
 LIMIT = 4 << 20
 COLS = 256
 VMEM = pl.BlockSpec(memory_space=pltpu.VMEM)
@@ -256,9 +258,10 @@
         slot = lax.rem(b - 1, n_buf)
         return pltpu.make_async_copy(wd.at[:, :, pl.ds(pl.multiple_of(b * COLS, COLS), COLS)], wd_buf.at[slot], w_sem.at[slot])
 
-    for b in range(1, n_buf + 1):
-        load(b).start()
-    entry_barrier(me)
+    load(1).start()
+    barrier = pltpu.get_barrier_semaphore()
+    for d in range(1, N_DEV):
+        pl.semaphore_signal(barrier, inc=1, device_id={"ep": lax.rem(me + d, N_DEV)}, device_id_type=MESH)
 
     def send_d2d(b):
         return remote(part.at[b, 1 - core], d2d.at[b], ds.at[b], dr.at[b], sib)
@@ -309,48 +312,46 @@
         for i in range(N_DEV):
             o[i, pl.ds(e * CAP, CAP), :] = out[i * CAP : (i + 1) * CAP]
 
-    def on_weights(b, body):
-        @pl.when(b == 0)
-        def _():
-            body(wd_on)
-
-        @pl.when((b >= 1) & (b < n_blk))
-        def _():
-            body(wd_buf.at[lax.rem(b - 1, n_buf)])
+    def front(b, weights):
+        for e in range(FRONT):
+            down(e, weights)
+
+        @pl.when(b + 2 < n_blk)
+        def _():
+            load(b + 2).start()
+
+    def back(b, weights):
+        for e in range(FRONT, n_exp):
+            down(e, weights)
+        for i in range(N_DEV):
+            gates = s[i // 2, :, pl.ds((i % 2) * 64, 64), :].reshape(192, 256)
+            terms = jnp.dot(gates, o[i], preferred_element_type=F32)
+            part[b, i % 2, i // 4, (i // 2) % 2] = terms[0:64] + terms[64:128] + terms[128:192]
+
+    front(0, wd_on)
+    back(0, wd_on)
+    pl.semaphore_wait(barrier, N_DEV - 1)
 
     def step(b, carry):
         lag(b, 1, stage_1)
-
-        @pl.when((b >= 1) & (b < n_blk))
+        weights = wd_buf.at[lax.rem(b - 1, n_buf)]
+
+        @pl.when(b < n_blk)
         def _():
             load(b).wait()
-
-        def front(weights):
-            for e in range(FRONT):
-                down(e, weights)
-
-        on_weights(b, front)
+            front(b, weights)
+
         lag(b, 1, stage_2)
-        lag(b, 3, stage_3)
-        lag(b, 5, stage_4)
-
-        def back(weights):
-            for e in range(FRONT, n_exp):
-                down(e, weights)
-            for i in range(N_DEV):
-                gates = s[i // 2, :, pl.ds((i % 2) * 64, 64), :].reshape(192, 256)
-                terms = jnp.dot(gates, o[i], preferred_element_type=F32)
-                part[b, i % 2, i // 4, (i // 2) % 2] = terms[0:64] + terms[64:128] + terms[128:192]
-
-        on_weights(b, back)
-
-        @pl.when((b >= 1) & (b + n_buf < n_blk))
-        def _():
-            load(b + n_buf).start()
+        lag(b, LAG_3, stage_3)
+        lag(b, LAG_4, stage_4)
+
+        @pl.when(b < n_blk)
+        def _():
+            back(b, weights)
 
         return carry
 
-    lax.fori_loop(0, n_blk + 5, step, 0)
+    lax.fori_loop(1, n_blk + LAG_4, step, 0)
 
     def drain(b, carry):
         for send in (send_d2d, send_1a, send_1b, send_2a, send_2b):

time: 68.3 us -> 66.6 us (0.975)
  Pallas kernels: 67.4 us -> 65.8 us
    pallas_call x1, Pallas kernels: 21.6 us -> 20 us  [local_step(): pl.pallas_call(hidden_kernel, out_shape=[on_chip(w_on.shape, BF16), on_ch...]
where the time goes in v5:
time: 66.6 us; the launch traced here: 66.5 us
  Pallas kernels  65.8 us (99%)
  local copies, waits for them, and re-layouts  0.71 us (1%)
    pallas_call x1, Pallas kernels, local_step(): pl.pallas_call(combine_kernel, out_shape=jax.ShapeDtypeStruct((n_tok, d_m...  29.1 us
    pallas_call x1, Pallas kernels, local_step(): pl.pallas_call(hidden_kernel, out_shape=[on_chip(w_on.shape, BF16), on_ch...  20 us
    pallas_call x1, Pallas kernels, local_step(): pl.pallas_call(gather_kernel, out_shape=[on_chip((SLOTS, 2, d_model, d_ff...  16.6 us

profile of v5, /device:TPU:0, one launch (start us, length us, event | category | flops | bytes accessed | tf_op | source)
XLA Modules:
  0.0 66.5 jit_solution(17394209115691788280)
XLA Ops:
  0.0 16.6 %gather.1 = (bf16[4,2,2048,1408]{3,2,1,0:T(8,128)(2,1)S(1)}, bf16[512,2048]{1,0:T(8,128)(2,1)S(1)}, f32[8,512]{1,0:T(8,128)S(1)}, bf16[8,256,1408]{2,1,0:T(8,128...) custom-call(bf16[64,2048]{1,0:T(8,128)(2,1)} %tok.1, s32[6,64]{1,0:T(8,128)} %bitcast.2, ...), custom_call_target="tpu_custom_call" | custom-call | tf_op jit(solution)/shard_map/gather/pallas_call | solution.py:374
  16.6 20.0 %hidden.1 = (bf16[4,2,2048,1408]{3,2,1,0:T(8,128)(2,1)S(1)}, bf16[8,256,1408]{2,1,0:T(8,128)(2,1)S(1)}, bf16[8,1408,256]{2,1,0:T(8,128)(2,1)S(1)}) custom-call(bf16[4,2,2048,1408]{3,2,1,0:T(8,128)(2,1)S(1)} %get-tuple-element.13.w_in, bf16[8,256,1408]{2,1,0:T(8,128)(2,1)S(1)} %get-tuple-element.14.h_in, ...), custom_call_target="tpu_custom_call", output_to_operand_aliasing={{0}: (0, {}), {1}: (1, {}), {2}: (2, {})} | custom-call | tf_op jit(solution)/shard_map/hidden/pallas_call | solution.py:397
  36.6 29.1 %combine.1 = bf16[64,2048]{1,0:T(8,128)(2,1)S(1)} custom-call(bf16[8,256,1408]{2,1,0:T(8,128)(2,1)S(1)} %get-tuple-element.18.h, bf16[4,3,128,256]{3,2,1,0:T(8,128)(2,1)S(1)} %get-tuple-element.19.s, bf16[8,1408,256]{2,1,0:T(8,128)(2,1)S(1)} %get-tuple-element.20.wd_on, bf16[8,1408,2048]{2,1,0:T(8,128)(2,1)} %wd.3), custom_call_target="tpu_custom_call" | custom-call | tf_op jit(solution)/shard_map/combine/pallas_call | solution.py:407
  65.8 0.7 %copy.14 = bf16[64,2048]{1,0:T(8,128)(2,1)} copy(bf16[64,2048]{1,0:T(8,128)(2,1)S(1)} %combine.1) | data formatting | bytes 524288

commit v6 on v5

--- a/solution.py
+++ b/solution.py
@@ -11,7 +11,7 @@
 N_DEV = 8
 CAP = 32
 SLOTS = 4
-EARLY = 3
+WAITS = (0, 3)
 FRONT = 6
 LAG_3 = 3
 LAG_4 = 6
@@ -66,7 +66,7 @@
     for d in range(1, N_DEV):
         pl.semaphore_signal(barrier, inc=1, device_id={"ep": lax.rem(me + d, N_DEV)}, device_id_type=MESH)
     loads = []
-    for e in range(EARLY):
+    for e in range(SLOTS):
         loads.append(pltpu.make_async_copy(wg.at[e], w_out.at[e, 0], w_sem.at[e, 0]))
         loads.append(pltpu.make_async_copy(wu.at[e], w_out.at[e, 1], w_sem.at[e, 1]))
     for load in loads:
@@ -170,18 +170,18 @@
 def hidden_kernel(w_in, h_in, wd_in, x_all, codes, wg, wu, wd, w_buf, h_out, wd_out, xe, w_sem, d_sem):
     n_exp = wg.shape[0]
     d_ff = wg.shape[2]
-
-    def load(e, part, src):
-        s = lax.rem(e, SLOTS)
-        return pltpu.make_async_copy(src.at[e], w_buf.at[s, part], w_sem.at[s, part])
-
-    for e in range(EARLY, SLOTS):
-        load(e, 0, wg).start()
-        load(e, 1, wu).start()
+    panels = [(c, min(256, d_ff - c)) for c in range(0, d_ff, 256)]
     down = pltpu.make_async_copy(wd.at[:, :, pl.ds(0, COLS)], wd_out, d_sem)
 
-    def hidden_rows(e, cap, slot):
+    def load(e, p):
+        c, w = panels[p]
+        slot = lax.rem(e, SLOTS)
+        cols = pl.ds(c, w)
+        return [pltpu.make_async_copy(src.at[e, :, cols], w_buf.at[slot, part, :, cols], w_sem.at[slot, part, p]) for part, src in ((0, wg), (1, wu))]
+
+    def hidden_rows(e, cap, before, after):
         m = cap * N_DEV
+        slot = lax.rem(e, SLOTS)
         r = lax.broadcasted_iota(jnp.int32, (m, 512), 0)
         target = ((r // cap) * CAP + lax.rem(r, cap) + 1).astype(F32)
         pick = (target == codes[pl.ds(e, 1), :]).astype(BF16)
@@ -189,7 +189,8 @@
             part = jnp.dot(pick, x_all[:, pl.ds(c, 512)], preferred_element_type=F32)
             xe[pl.ds(0, m), pl.ds(c, 512)] = part.astype(BF16)
 
-        def put(act, c, w):
+        def put(a, b, c, w):
+            act = (a * jax.nn.sigmoid(a) * b).astype(BF16)
             if cap == CAP:
                 h_out[e, :, pl.ds(c, w)] = act
             else:
@@ -197,52 +198,56 @@
                     h_out[e, pl.ds(i * CAP, cap), pl.ds(c, w)] = act[i * cap : (i + 1) * cap]
                     h_out[e, pl.ds(i * CAP + cap, CAP - cap), pl.ds(c, w)] = jnp.zeros((CAP - cap, w), BF16)
 
-        def act_of(a, b):
-            return (a * jax.nn.sigmoid(a) * b).astype(BF16)
-
         rows = xe[pl.ds(0, m), :]
-        for c in range(0, d_ff - 128, 256):
-            a = jnp.dot(rows, w_buf[slot, 0, :, pl.ds(c, 256)], preferred_element_type=F32)
-            b = jnp.dot(rows, w_buf[slot, 1, :, pl.ds(c, 256)], preferred_element_type=F32)
-            put(act_of(a, b), c, 256)
-        c = d_ff - 128
-        both = jnp.concatenate([w_buf[slot, 0, :, pl.ds(c, 128)], w_buf[slot, 1, :, pl.ds(c, 128)]], axis=1)
-        ab = jnp.dot(rows, both, preferred_element_type=F32)
-        put(act_of(ab[:, :128], ab[:, 128:]), c, 128)
-
-    def step(e, carry):
-        slot = lax.rem(e, SLOTS)
-
-        @pl.when(e >= EARLY)
-        def _():
-            load(e, 0, wg).wait()
-            load(e, 1, wu).wait()
-
+        for p, (c, w) in enumerate(panels):
+            before(e, p)
+            if w == 256:
+                a = jnp.dot(rows, w_buf[slot, 0, :, pl.ds(c, w)], preferred_element_type=F32)
+                b = jnp.dot(rows, w_buf[slot, 1, :, pl.ds(c, w)], preferred_element_type=F32)
+            else:
+                both = jnp.concatenate([w_buf[slot, 0, :, pl.ds(c, w)], w_buf[slot, 1, :, pl.ds(c, w)]], axis=1)
+                ab = jnp.dot(rows, both, preferred_element_type=F32)
+                a, b = ab[:, :w], ab[:, w:]
+            put(a, b, c, w)
+            after(e, p)
+
+    def expert(e, before, after):
         code_row = codes[pl.ds(e, 1), :]
         block = lax.broadcasted_iota(jnp.int32, (1, 512), 1) // 64
-        most = jnp.max(code_row - (block * CAP).astype(F32))
-        small = most <= 16.0
+        small = jnp.max(code_row - (block * CAP).astype(F32)) <= 16.0
 
         @pl.when(small)
         def _():
-            hidden_rows(e, CAP // 2, slot)
+            hidden_rows(e, CAP // 2, before, after)
 
         @pl.when(jnp.logical_not(small))
         def _():
-            hidden_rows(e, CAP, slot)
-
-        @pl.when(e + SLOTS < n_exp)
-        def _():
-            load(e + SLOTS, 0, wg).start()
-            load(e + SLOTS, 1, wu).start()
-
-        @pl.when(e + SLOTS == n_exp)
-        def _():
-            down.start()
-
+            hidden_rows(e, CAP, before, after)
+
+    def nothing(e, p):
+        pass
+
+    def refill(e, p):
+        for copy in load(e + SLOTS, p):
+            copy.start()
+
+    def arrive(e, p):
+        if p in WAITS:
+            for q in range(p, min([v for v in WAITS if v > p] + [len(panels)])):
+                for copy in load(e, q):
+                    copy.wait()
+
+    def early(e, carry):
+        expert(e, nothing, refill)
         return carry
 
-    lax.fori_loop(0, n_exp, step, 0)
+    def late(e, carry):
+        expert(e, arrive, nothing)
+        return carry
+
+    lax.fori_loop(0, SLOTS, early, 0)
+    down.start()
+    lax.fori_loop(SLOTS, n_exp, late, 0)
     down.wait()
 
 
@@ -382,7 +387,7 @@
                 pltpu.VMEM((2, 8, 128), F32),
                 pltpu.VMEM((N_DEV, 16, 128), F32),
                 pltpu.VMEM((N_DEV, 16, 128), F32),
-                dma((EARLY, 2)),
+                dma((SLOTS, 2)),
                 dma((3,)),
                 dma((7,)),
                 dma((7,)),
@@ -399,7 +404,7 @@
             out_shape=[on_chip(w_on.shape, BF16), on_chip(hidden, BF16), on_chip(wd_on.shape, BF16)],
             in_specs=[VMEM] * 5 + [ANY] * 3,
             out_specs=[VMEM] * 3,
-            scratch_shapes=[pltpu.VMEM((256, d_model), BF16), dma((SLOTS, 2)), dma],
+            scratch_shapes=[pltpu.VMEM((256, d_model), BF16), dma((SLOTS, 2, 6)), dma],
             input_output_aliases={0: 0, 1: 1, 2: 2},
             compiler_params=pltpu.CompilerParams(vmem_limit_bytes=LIMIT),
             name="hidden",

time: 66.6 us -> 70.3 us (1.056)
  Pallas kernels: 65.8 us -> 69 us
    pallas_call x1, Pallas kernels: 29.1 us -> 31.2 us  [local_step(): pl.pallas_call(combine_kernel, out_shape=jax.ShapeDtypeStruct((n_tok, d_m...]
    pallas_call x1, Pallas kernels: 20 us -> 21.1 us  [local_step(): pl.pallas_call(hidden_kernel, out_shape=[on_chip(w_on.shape, BF16), on_ch...]
where the time goes in v6:
time: 70.3 us; the launch traced here: 69.7 us
  Pallas kernels  69 us (98%)
  local copies, waits for them, and re-layouts  0.71 us (1%)
    pallas_call x1, Pallas kernels, local_step(): pl.pallas_call(combine_kernel, out_shape=jax.ShapeDtypeStruct((n_tok, d_m...  31.2 us
    pallas_call x1, Pallas kernels, local_step(): pl.pallas_call(hidden_kernel, out_shape=[on_chip(w_on.shape, BF16), on_ch...  21.1 us
    pallas_call x1, Pallas kernels, local_step(): pl.pallas_call(gather_kernel, out_shape=[on_chip((SLOTS, 2, d_model, d_ff...  16.6 us

profile of v6, /device:TPU:0, one launch (start us, length us, event | category | flops | bytes accessed | tf_op | source)
XLA Modules:
  0.0 69.7 jit_solution(11694626997733573482)
XLA Ops:
  0.0 16.6 %gather.1 = (bf16[4,2,2048,1408]{3,2,1,0:T(8,128)(2,1)S(1)}, bf16[512,2048]{1,0:T(8,128)(2,1)S(1)}, f32[8,512]{1,0:T(8,128)S(1)}, bf16[8,256,1408]{2,1,0:T(8,128...) custom-call(bf16[64,2048]{1,0:T(8,128)(2,1)} %tok.1, s32[6,64]{1,0:T(8,128)} %bitcast.2, ...), custom_call_target="tpu_custom_call" | custom-call | tf_op jit(solution)/shard_map/gather/pallas_call | solution.py:379
  16.6 21.1 %hidden.1 = (bf16[4,2,2048,1408]{3,2,1,0:T(8,128)(2,1)S(1)}, bf16[8,256,1408]{2,1,0:T(8,128)(2,1)S(1)}, bf16[8,1408,256]{2,1,0:T(8,128)(2,1)S(1)}) custom-call(bf16[4,2,2048,1408]{3,2,1,0:T(8,128)(2,1)S(1)} %get-tuple-element.13.w_in, bf16[8,256,1408]{2,1,0:T(8,128)(2,1)S(1)} %get-tuple-element.14.h_in, ...), custom_call_target="tpu_custom_call", output_to_operand_aliasing={{0}: (0, {}), {1}: (1, {}), {2}: (2, {})} | custom-call | tf_op jit(solution)/shard_map/hidden/pallas_call | solution.py:402
  37.8 31.2 %combine.1 = bf16[64,2048]{1,0:T(8,128)(2,1)S(1)} custom-call(bf16[8,256,1408]{2,1,0:T(8,128)(2,1)S(1)} %get-tuple-element.18.h, bf16[4,3,128,256]{3,2,1,0:T(8,128)(2,1)S(1)} %get-tuple-element.19.s, bf16[8,1408,256]{2,1,0:T(8,128)(2,1)S(1)} %get-tuple-element.20.wd_on, bf16[8,1408,2048]{2,1,0:T(8,128)(2,1)} %wd.3), custom_call_target="tpu_custom_call" | custom-call | tf_op jit(solution)/shard_map/combine/pallas_call | solution.py:412
  69.0 0.7 %copy.14 = bf16[64,2048]{1,0:T(8,128)(2,1)} copy(bf16[64,2048]{1,0:T(8,128)(2,1)S(1)} %combine.1) | data formatting | bytes 524288

commit v7 on v6

--- a/solution.py
+++ b/solution.py
@@ -11,7 +11,7 @@
 N_DEV = 8
 CAP = 32
 SLOTS = 4
-WAITS = (0, 3)
+SPLIT = 768
 FRONT = 6
 LAG_3 = 3
 LAG_4 = 6
@@ -174,9 +174,8 @@
     down = pltpu.make_async_copy(wd.at[:, :, pl.ds(0, COLS)], wd_out, d_sem)
 
     def load(e, p):
-        c, w = panels[p]
         slot = lax.rem(e, SLOTS)
-        cols = pl.ds(c, w)
+        cols = pl.ds(p * SPLIT, SPLIT if p == 0 else d_ff - SPLIT)
         return [pltpu.make_async_copy(src.at[e, :, cols], w_buf.at[slot, part, :, cols], w_sem.at[slot, part, p]) for part, src in ((0, wg), (1, wu))]
 
     def hidden_rows(e, cap, before, after):
@@ -228,14 +227,14 @@
         pass
 
     def refill(e, p):
-        for copy in load(e + SLOTS, p):
-            copy.start()
+        if panels[p][0] + 256 == SPLIT or p == len(panels) - 1:
+            for copy in load(e + SLOTS, p // 3):
+                copy.start()
 
     def arrive(e, p):
-        if p in WAITS:
-            for q in range(p, min([v for v in WAITS if v > p] + [len(panels)])):
-                for copy in load(e, q):
-                    copy.wait()
+        if panels[p][0] in (0, SPLIT):
+            for copy in load(e, p // 3):
+                copy.wait()
 
     def early(e, carry):
         expert(e, nothing, refill)
@@ -245,25 +244,27 @@
         expert(e, arrive, nothing)
         return carry
 
+    down.start()
     lax.fori_loop(0, SLOTS, early, 0)
-    down.start()
     lax.fori_loop(SLOTS, n_exp, late, 0)
     down.wait()
 
 
-def combine_kernel(h, s, wd_on, wd, y_out, wd_buf, o, part, d2d, h1a, h1b, h2a, h2b, w_sem, ds, dr, h1as, h1ar, h1bs, h1br, h2as, h2ar, h2bs, h2br):
+def combine_kernel(h, s, wd_on, wd, y_out, wd_one, wd_pair, o, part, d2d, h1a, h1b, h2a, h2b, one_sem, pair_sem, ds, dr, h1as, h1ar, h1bs, h1br, h2as, h2ar, h2bs, h2br):
     me, core, x, y, sib, xn, yn = place()
     n_blk = wd.shape[2] // COLS
-    n_buf = wd_buf.shape[0]
     n_exp = h.shape[0]
     half = 32
     first, second = pl.ds(0, half), pl.ds(half, half)
 
-    def load(b):
-        slot = lax.rem(b - 1, n_buf)
-        return pltpu.make_async_copy(wd.at[:, :, pl.ds(pl.multiple_of(b * COLS, COLS), COLS)], wd_buf.at[slot], w_sem.at[slot])
-
-    load(1).start()
+    one = pltpu.make_async_copy(wd.at[:, :, pl.ds(COLS, COLS)], wd_one, one_sem)
+
+    def pair(q):
+        cols = pl.ds(pl.multiple_of((q + 1) * 2 * COLS, 2 * COLS), 2 * COLS)
+        slot = lax.rem(q, 2)
+        return pltpu.make_async_copy(wd.at[:, :, cols], wd_pair.at[slot], pair_sem.at[slot])
+
+    one.start()
     barrier = pltpu.get_barrier_semaphore()
     for d in range(1, N_DEV):
         pl.semaphore_signal(barrier, inc=1, device_id={"ep": lax.rem(me + d, N_DEV)}, device_id_type=MESH)
@@ -317,13 +318,9 @@
         for i in range(N_DEV):
             o[i, pl.ds(e * CAP, CAP), :] = out[i * CAP : (i + 1) * CAP]
 
-    def front(b, weights):
+    def front(weights):
         for e in range(FRONT):
             down(e, weights)
-
-        @pl.when(b + 2 < n_blk)
-        def _():
-            load(b + 2).start()
 
     def back(b, weights):
         for e in range(FRONT, n_exp):
@@ -333,18 +330,30 @@
             terms = jnp.dot(gates, o[i], preferred_element_type=F32)
             part[b, i % 2, i // 4, (i // 2) % 2] = terms[0:64] + terms[64:128] + terms[128:192]
 
-    front(0, wd_on)
+    front(wd_on)
+    pair(0).start()
     back(0, wd_on)
     pl.semaphore_wait(barrier, N_DEV - 1)
+    stage_1(0)
+    one.wait()
+    front(wd_one)
+    stage_2(0)
+    pair(1).start()
+    back(1, wd_one)
 
     def step(b, carry):
         lag(b, 1, stage_1)
-        weights = wd_buf.at[lax.rem(b - 1, n_buf)]
+        q = (b - 2) // 2
+        cols = pl.ds(pl.multiple_of(lax.rem(b, 2) * COLS, COLS), COLS)
+        weights = wd_pair.at[lax.rem(q, 2), :, :, cols]
+
+        @pl.when((b < n_blk) & (lax.rem(b, 2) == 0))
+        def _():
+            pair(q).wait()
 
         @pl.when(b < n_blk)
         def _():
-            load(b).wait()
-            front(b, weights)
+            front(weights)
 
         lag(b, 1, stage_2)
         lag(b, LAG_3, stage_3)
@@ -354,9 +363,13 @@
         def _():
             back(b, weights)
 
+        @pl.when((lax.rem(b, 2) == 1) & (b + 4 < n_blk))
+        def _():
+            pair(q + 2).start()
+
         return carry
 
-    lax.fori_loop(1, n_blk + LAG_4, step, 0)
+    lax.fori_loop(2, n_blk + LAG_4, step, 0)
 
     def drain(b, carry):
         for send in (send_d2d, send_1a, send_1b, send_2a, send_2b):
@@ -404,7 +417,7 @@
             out_shape=[on_chip(w_on.shape, BF16), on_chip(hidden, BF16), on_chip(wd_on.shape, BF16)],
             in_specs=[VMEM] * 5 + [ANY] * 3,
             out_specs=[VMEM] * 3,
-            scratch_shapes=[pltpu.VMEM((256, d_model), BF16), dma((SLOTS, 2, 6)), dma],
+            scratch_shapes=[pltpu.VMEM((256, d_model), BF16), dma((SLOTS, 2, 2)), dma],
             input_output_aliases={0: 0, 1: 1, 2: 2},
             compiler_params=pltpu.CompilerParams(vmem_limit_bytes=LIMIT),
             name="hidden",
@@ -415,7 +428,8 @@
             in_specs=[VMEM] * 3 + [ANY],
             out_specs=VMEM,
             scratch_shapes=[
-                pltpu.VMEM((3, n_exp, d_ff, COLS), BF16),
+                pltpu.VMEM((n_exp, d_ff, COLS), BF16),
+                pltpu.VMEM((2, n_exp, d_ff, 2 * COLS), BF16),
                 pltpu.VMEM((N_DEV, 256, COLS), BF16),
                 pltpu.VMEM((n_blk, 2, 2, 2, n_tok, COLS), F32),
                 pltpu.VMEM((n_blk, 2, 2, n_tok, COLS), F32),
@@ -423,10 +437,11 @@
                 pltpu.VMEM((n_blk, 2, n_tok // 2, COLS), F32),
                 pltpu.VMEM((n_blk, n_tok // 2, COLS), F32),
                 pltpu.VMEM((n_blk, n_tok // 2, COLS), F32),
-                dma((3,)),
+                dma,
+                dma((2,)),
             ]
             + [dma((n_blk,))] * 10,
-            compiler_params=pltpu.CompilerParams(collective_id=1, has_side_effects=True, vmem_limit_bytes=32 << 20),
+            compiler_params=pltpu.CompilerParams(collective_id=1, has_side_effects=True, vmem_limit_bytes=38 << 20),
             name="combine",
         )(pin(h), pin(s), pin(wd_on), wd)
 

time: 70.3 us -> 70.1 us (level); the launches traced: 69.7 us -> 70.6 us
  Pallas kernels: 69 us -> 69.9 us
    pallas_call x1, Pallas kernels: 21.1 us -> 24.1 us  [local_step(): pl.pallas_call(hidden_kernel, out_shape=[on_chip(w_on.shape, BF16), on_ch...]
    pallas_call x1, Pallas kernels: 31.2 us -> 29.1 us  [local_step(): pl.pallas_call(combine_kernel, out_shape=jax.ShapeDtypeStruct((n_tok, d_m...]
where the time goes in v7:
time: 70.1 us; the launch traced here: 70.6 us
  Pallas kernels  69.9 us (100%)
  local copies, waits for them, and re-layouts  0.71 us (1%)
    pallas_call x1, Pallas kernels, local_step(): pl.pallas_call(combine_kernel, out_shape=jax.ShapeDtypeStruct((n_tok, d_m...  29.1 us
    pallas_call x1, Pallas kernels, local_step(): pl.pallas_call(hidden_kernel, out_shape=[on_chip(w_on.shape, BF16), on_ch...  24.1 us
    pallas_call x1, Pallas kernels, local_step(): pl.pallas_call(gather_kernel, out_shape=[on_chip((SLOTS, 2, d_model, d_ff...  16.6 us

profile of v7, /device:TPU:0, one launch (start us, length us, event | category | flops | bytes accessed | tf_op | source)
XLA Modules:
  0.0 70.6 jit_solution(17065825265314916132)
XLA Ops:
  0.0 16.6 %gather.1 = (bf16[4,2,2048,1408]{3,2,1,0:T(8,128)(2,1)S(1)}, bf16[512,2048]{1,0:T(8,128)(2,1)S(1)}, f32[8,512]{1,0:T(8,128)S(1)}, bf16[8,256,1408]{2,1,0:T(8,128...) custom-call(bf16[64,2048]{1,0:T(8,128)(2,1)} %tok.1, s32[6,64]{1,0:T(8,128)} %bitcast.2, ...), custom_call_target="tpu_custom_call" | custom-call | tf_op jit(solution)/shard_map/gather/pallas_call | solution.py:392
  16.6 24.1 %hidden.1 = (bf16[4,2,2048,1408]{3,2,1,0:T(8,128)(2,1)S(1)}, bf16[8,256,1408]{2,1,0:T(8,128)(2,1)S(1)}, bf16[8,1408,256]{2,1,0:T(8,128)(2,1)S(1)}) custom-call(bf16[4,2,2048,1408]{3,2,1,0:T(8,128)(2,1)S(1)} %get-tuple-element.13.w_in, bf16[8,256,1408]{2,1,0:T(8,128)(2,1)S(1)} %get-tuple-element.14.h_in, ...), custom_call_target="tpu_custom_call", output_to_operand_aliasing={{0}: (0, {}), {1}: (1, {}), {2}: (2, {})} | custom-call | tf_op jit(solution)/shard_map/hidden/pallas_call | solution.py:415
  40.7 29.1 %combine.1 = bf16[64,2048]{1,0:T(8,128)(2,1)S(1)} custom-call(bf16[8,256,1408]{2,1,0:T(8,128)(2,1)S(1)} %get-tuple-element.18.h, bf16[4,3,128,256]{3,2,1,0:T(8,128)(2,1)S(1)} %get-tuple-element.19.s, bf16[8,1408,256]{2,1,0:T(8,128)(2,1)S(1)} %get-tuple-element.20.wd_on, bf16[8,1408,2048]{2,1,0:T(8,128)(2,1)} %wd.3), custom_call_target="tpu_custom_call" | custom-call | tf_op jit(solution)/shard_map/combine/pallas_call | solution.py:425
  69.9 0.7 copy.14

commit v8 on v5

--- a/solution.py
+++ b/solution.py
@@ -10,8 +10,8 @@
 MESH = pl.DeviceIdType.MESH
 N_DEV = 8
 CAP = 32
-SLOTS = 4
-EARLY = 3
+SLOTS = 3
+AHEAD = 2
 FRONT = 6
 LAG_3 = 3
 LAG_4 = 6
@@ -48,7 +48,7 @@
     pl.semaphore_wait(barrier, N_DEV - 1)
 
 
-def gather_kernel(tok, route_t, gate_t, wg, wu, w_out, x_out, codes_out, h_out, s_out, wd_out, pad_i, pad_g, pad, sg_loc, sg, w_sem, in_sem, sib_s, sib_r, link_s, link_r, sg_s, sg_r):
+def gather_kernel(tok, route_t, gate_t, wg, wu, wd, w_out, x_out, codes_out, s_out, wd_out, h_out, o_out, pad_i, pad_g, pad, sg_loc, sg, w_sem, d_sem, in_sem, sib_s, sib_r, link_s, link_r, sg_s, sg_r):
     me, core, x, y, sib, xn, yn = place()
     n_tok = tok.shape[0]
     half = n_tok // 2
@@ -66,9 +66,10 @@
     for d in range(1, N_DEV):
         pl.semaphore_signal(barrier, inc=1, device_id={"ep": lax.rem(me + d, N_DEV)}, device_id_type=MESH)
     loads = []
-    for e in range(EARLY):
+    for e in range(SLOTS):
         loads.append(pltpu.make_async_copy(wg.at[e], w_out.at[e, 0], w_sem.at[e, 0]))
         loads.append(pltpu.make_async_copy(wu.at[e], w_out.at[e, 1], w_sem.at[e, 1]))
+    loads.append(pltpu.make_async_copy(wd.at[:, :, pl.ds(0, AHEAD * COLS)], wd_out, d_sem))
     for load in loads:
         load.start()
 
@@ -167,21 +168,18 @@
         load.wait()
 
 
-def hidden_kernel(w_in, h_in, wd_in, x_all, codes, wg, wu, wd, w_buf, h_out, wd_out, xe, w_sem, d_sem):
+def hidden_kernel(w_in, h_in, o_in, x_all, codes, wd_on, wg, wu, w_buf, h_out, o_out, xe, hc, w_sem):
     n_exp = wg.shape[0]
     d_ff = wg.shape[2]
+    panels = [(c, min(256, d_ff - c)) for c in range(0, d_ff, 256)]
 
     def load(e, part, src):
-        s = lax.rem(e, SLOTS)
-        return pltpu.make_async_copy(src.at[e], w_buf.at[s, part], w_sem.at[s, part])
-
-    for e in range(EARLY, SLOTS):
-        load(e, 0, wg).start()
-        load(e, 1, wu).start()
-    down = pltpu.make_async_copy(wd.at[:, :, pl.ds(0, COLS)], wd_out, d_sem)
-
-    def hidden_rows(e, cap, slot):
+        slot = lax.rem(e, SLOTS)
+        return pltpu.make_async_copy(src.at[e], w_buf.at[slot, part], w_sem.at[slot, part])
+
+    def hidden_rows(e, cap):
         m = cap * N_DEV
+        slot = lax.rem(e, SLOTS)
         r = lax.broadcasted_iota(jnp.int32, (m, 512), 0)
         target = ((r // cap) * CAP + lax.rem(r, cap) + 1).astype(F32)
         pick = (target == codes[pl.ds(e, 1), :]).astype(BF16)
@@ -189,7 +187,17 @@
             part = jnp.dot(pick, x_all[:, pl.ds(c, 512)], preferred_element_type=F32)
             xe[pl.ds(0, m), pl.ds(c, 512)] = part.astype(BF16)
 
-        def put(act, c, w):
+        rows = xe[pl.ds(0, m), :]
+        for c, w in panels:
+            if w == 256:
+                a = jnp.dot(rows, w_buf[slot, 0, :, pl.ds(c, w)], preferred_element_type=F32)
+                b = jnp.dot(rows, w_buf[slot, 1, :, pl.ds(c, w)], preferred_element_type=F32)
+            else:
+                both = jnp.concatenate([w_buf[slot, 0, :, pl.ds(c, w)], w_buf[slot, 1, :, pl.ds(c, w)]], axis=1)
+                ab = jnp.dot(rows, both, preferred_element_type=F32)
+                a, b = ab[:, :w], ab[:, w:]
+            act = (a * jax.nn.sigmoid(a) * b).astype(BF16)
+            hc[pl.ds(0, m), pl.ds(c, w)] = act
             if cap == CAP:
                 h_out[e, :, pl.ds(c, w)] = act
             else:
@@ -197,68 +205,56 @@
                     h_out[e, pl.ds(i * CAP, cap), pl.ds(c, w)] = act[i * cap : (i + 1) * cap]
                     h_out[e, pl.ds(i * CAP + cap, CAP - cap), pl.ds(c, w)] = jnp.zeros((CAP - cap, w), BF16)
 
-        def act_of(a, b):
-            return (a * jax.nn.sigmoid(a) * b).astype(BF16)
-
-        rows = xe[pl.ds(0, m), :]
-        for c in range(0, d_ff - 128, 256):
-            a = jnp.dot(rows, w_buf[slot, 0, :, pl.ds(c, 256)], preferred_element_type=F32)
-            b = jnp.dot(rows, w_buf[slot, 1, :, pl.ds(c, 256)], preferred_element_type=F32)
-            put(act_of(a, b), c, 256)
-        c = d_ff - 128
-        both = jnp.concatenate([w_buf[slot, 0, :, pl.ds(c, 128)], w_buf[slot, 1, :, pl.ds(c, 128)]], axis=1)
-        ab = jnp.dot(rows, both, preferred_element_type=F32)
-        put(act_of(ab[:, :128], ab[:, 128:]), c, 128)
+        at = pl.multiple_of(e * CAP, CAP)
+        out = jnp.dot(hc[pl.ds(0, m), :], wd_on[e], preferred_element_type=F32).astype(BF16)
+        for k in range(AHEAD):
+            for i in range(N_DEV):
+                o_out[k, i, pl.ds(at, cap), :] = out[i * cap : (i + 1) * cap, k * COLS : (k + 1) * COLS]
+                if cap < CAP:
+                    o_out[k, i, pl.ds(at + cap, CAP - cap), :] = jnp.zeros((CAP - cap, COLS), BF16)
 
     def step(e, carry):
-        slot = lax.rem(e, SLOTS)
-
-        @pl.when(e >= EARLY)
+        @pl.when(e >= SLOTS)
         def _():
             load(e, 0, wg).wait()
             load(e, 1, wu).wait()
 
         code_row = codes[pl.ds(e, 1), :]
         block = lax.broadcasted_iota(jnp.int32, (1, 512), 1) // 64
-        most = jnp.max(code_row - (block * CAP).astype(F32))
-        small = most <= 16.0
+        small = jnp.max(code_row - (block * CAP).astype(F32)) <= 16.0
 
         @pl.when(small)
         def _():
-            hidden_rows(e, CAP // 2, slot)
+            hidden_rows(e, CAP // 2)
 
         @pl.when(jnp.logical_not(small))
         def _():
-            hidden_rows(e, CAP, slot)
+            hidden_rows(e, CAP)
 
         @pl.when(e + SLOTS < n_exp)
         def _():
             load(e + SLOTS, 0, wg).start()
             load(e + SLOTS, 1, wu).start()
 
-        @pl.when(e + SLOTS == n_exp)
-        def _():
-            down.start()
-
         return carry
 
     lax.fori_loop(0, n_exp, step, 0)
-    down.wait()
-
-
-def combine_kernel(h, s, wd_on, wd, y_out, wd_buf, o, part, d2d, h1a, h1b, h2a, h2b, w_sem, ds, dr, h1as, h1ar, h1bs, h1br, h2as, h2ar, h2bs, h2br):
+
+
+def combine_kernel(h, s, o_on, wd, y_out, wd_buf, o, part, d2d, h1a, h1b, h2a, h2b, w_sem, ds, dr, h1as, h1ar, h1bs, h1br, h2as, h2ar, h2bs, h2br):
     me, core, x, y, sib, xn, yn = place()
     n_blk = wd.shape[2] // COLS
-    n_buf = wd_buf.shape[0]
     n_exp = h.shape[0]
     half = 32
     first, second = pl.ds(0, half), pl.ds(half, half)
 
+    n_buf = wd_buf.shape[0]
+
     def load(b):
-        slot = lax.rem(b - 1, n_buf)
+        slot = lax.rem(b - AHEAD, n_buf)
         return pltpu.make_async_copy(wd.at[:, :, pl.ds(pl.multiple_of(b * COLS, COLS), COLS)], wd_buf.at[slot], w_sem.at[slot])
 
-    load(1).start()
+    load(AHEAD).start()
     barrier = pltpu.get_barrier_semaphore()
     for d in range(1, N_DEV):
         pl.semaphore_signal(barrier, inc=1, device_id={"ep": lax.rem(me + d, N_DEV)}, device_id_type=MESH)
@@ -312,46 +308,54 @@
         for i in range(N_DEV):
             o[i, pl.ds(e * CAP, CAP), :] = out[i * CAP : (i + 1) * CAP]
 
-    def front(b, weights):
-        for e in range(FRONT):
-            down(e, weights)
-
-        @pl.when(b + 2 < n_blk)
-        def _():
-            load(b + 2).start()
-
-    def back(b, weights):
-        for e in range(FRONT, n_exp):
-            down(e, weights)
+    def gather_sum(b, out):
         for i in range(N_DEV):
             gates = s[i // 2, :, pl.ds((i % 2) * 64, 64), :].reshape(192, 256)
-            terms = jnp.dot(gates, o[i], preferred_element_type=F32)
+            terms = jnp.dot(gates, out[i], preferred_element_type=F32)
             part[b, i % 2, i // 4, (i // 2) % 2] = terms[0:64] + terms[64:128] + terms[128:192]
 
-    front(0, wd_on)
-    back(0, wd_on)
+    gather_sum(0, o_on.at[0])
     pl.semaphore_wait(barrier, N_DEV - 1)
+    stage_1(0)
+    gather_sum(1, o_on.at[1])
+    stage_1(1)
+    load(AHEAD + 1).start()
+    stage_2(0)
+    stage_2(1)
 
     def step(b, carry):
-        lag(b, 1, stage_1)
-        weights = wd_buf.at[lax.rem(b - 1, n_buf)]
+        @pl.when((b > AHEAD) & (b < n_blk + 1))
+        def _():
+            stage_1(b - 1)
+
+        weights = wd_buf.at[lax.rem(b - AHEAD, n_buf)]
 
         @pl.when(b < n_blk)
         def _():
             load(b).wait()
-            front(b, weights)
-
-        lag(b, 1, stage_2)
+            for e in range(FRONT):
+                down(e, weights)
+
+        @pl.when(b + 2 < n_blk)
+        def _():
+            load(b + 2).start()
+
+        @pl.when((b > AHEAD) & (b < n_blk + 1))
+        def _():
+            stage_2(b - 1)
+
         lag(b, LAG_3, stage_3)
         lag(b, LAG_4, stage_4)
 
         @pl.when(b < n_blk)
         def _():
-            back(b, weights)
+            for e in range(FRONT, n_exp):
+                down(e, weights)
+            gather_sum(b, o)
 
         return carry
 
-    lax.fori_loop(1, n_blk + LAG_4, step, 0)
+    lax.fori_loop(AHEAD, n_blk + LAG_4, step, 0)
 
     def drain(b, carry):
         for send in (send_d2d, send_1a, send_1b, send_2a, send_2b):
@@ -371,18 +375,20 @@
         n_tok = tok.shape[0]
         n_blk = d_model // COLS
         hidden = (n_exp, N_DEV * CAP, d_ff)
-        w_on, x_all, codes, h, s, wd_on = pl.pallas_call(
+        down_2, rows_2 = (n_exp, d_ff, AHEAD * COLS), (AHEAD, N_DEV, 256, COLS)
+        w_on, x_all, codes, s, wd_on, h, o_on = pl.pallas_call(
             gather_kernel,
-            out_shape=[on_chip((SLOTS, 2, d_model, d_ff), BF16), on_chip((N_DEV * n_tok, d_model), BF16), on_chip((8, 512), F32), on_chip(hidden, BF16), on_chip((4, 3, 128, 256), BF16), on_chip((n_exp, d_ff, COLS), BF16)],
-            in_specs=[ANY] * 5,
-            out_specs=[VMEM] * 6,
+            out_shape=[on_chip((SLOTS, 2, d_model, d_ff), BF16), on_chip((N_DEV * n_tok, d_model), BF16), on_chip((8, 512), F32), on_chip((4, 3, 128, 256), BF16), on_chip(down_2, BF16), on_chip(hidden, BF16), on_chip(rows_2, BF16)],
+            in_specs=[ANY] * 6,
+            out_specs=[VMEM] * 7,
             scratch_shapes=[
                 pltpu.VMEM((6, n_tok), jnp.int32),
                 pltpu.VMEM((6, n_tok), F32),
                 pltpu.VMEM((2, 8, 128), F32),
                 pltpu.VMEM((N_DEV, 16, 128), F32),
                 pltpu.VMEM((N_DEV, 16, 128), F32),
-                dma((EARLY, 2)),
+                dma((SLOTS, 2)),
+                dma,
                 dma((3,)),
                 dma((7,)),
                 dma((7,)),
@@ -393,17 +399,17 @@
             ],
             compiler_params=pltpu.CompilerParams(collective_id=0, has_side_effects=True, vmem_limit_bytes=LIMIT),
             name="gather",
-        )(tok, route.T, gate.T, wg, wu)
-        unused, h, wd_on = pl.pallas_call(
+        )(tok, route.T, gate.T, wg, wu, wd)
+        unused, h, o_on = pl.pallas_call(
             hidden_kernel,
-            out_shape=[on_chip(w_on.shape, BF16), on_chip(hidden, BF16), on_chip(wd_on.shape, BF16)],
-            in_specs=[VMEM] * 5 + [ANY] * 3,
+            out_shape=[on_chip(w_on.shape, BF16), on_chip(hidden, BF16), on_chip(rows_2, BF16)],
+            in_specs=[VMEM] * 6 + [ANY] * 2,
             out_specs=[VMEM] * 3,
-            scratch_shapes=[pltpu.VMEM((256, d_model), BF16), dma((SLOTS, 2)), dma],
+            scratch_shapes=[pltpu.VMEM((256, d_model), BF16), pltpu.VMEM((256, d_ff), BF16), dma((SLOTS, 2))],
             input_output_aliases={0: 0, 1: 1, 2: 2},
             compiler_params=pltpu.CompilerParams(vmem_limit_bytes=LIMIT),
             name="hidden",
-        )(pin(w_on), pin(h), pin(wd_on), pin(x_all), pin(codes), wg, wu, wd)
+        )(pin(w_on), pin(h), pin(o_on), pin(x_all), pin(codes), pin(wd_on), wg, wu)
         return pl.pallas_call(
             combine_kernel,
             out_shape=jax.ShapeDtypeStruct((n_tok, d_model), BF16),
@@ -421,8 +427,8 @@
                 dma((3,)),
             ]
             + [dma((n_blk,))] * 10,
-            compiler_params=pltpu.CompilerParams(collective_id=1, has_side_effects=True, vmem_limit_bytes=32 << 20),
+            compiler_params=pltpu.CompilerParams(collective_id=1, has_side_effects=True, vmem_limit_bytes=29 << 20),
             name="combine",
-        )(pin(h), pin(s), pin(wd_on), wd)
+        )(pin(h), pin(s), pin(o_on), wd)
 
     return jax.shard_map(local_step, mesh=mesh, in_specs=(row_spec, row_spec, row_spec, expert_spec, expert_spec, expert_spec), out_specs=row_spec, check_vma=False)

time: 66.6 us -> 70.1 us (1.053)
  Pallas kernels: 65.8 us -> 69.6 us
    pallas_call x1, Pallas kernels: 20 us -> 24 us  [local_step(): pl.pallas_call(hidden_kernel, out_shape=[on_chip(w_on.shape, BF16), on_ch...]
where the time goes in v8:
time: 70.1 us; the launch traced here: 70.4 us
  Pallas kernels  69.6 us (99%)
  local copies, waits for them, and re-layouts  0.71 us (1%)
    pallas_call x1, Pallas kernels, local_step(): pl.pallas_call(combine_kernel, out_shape=jax.ShapeDtypeStruct((n_tok, d_m...  29 us
    pallas_call x1, Pallas kernels, local_step(): pl.pallas_call(hidden_kernel, out_shape=[on_chip(w_on.shape, BF16), on_ch...  24 us
    pallas_call x1, Pallas kernels, local_step(): pl.pallas_call(gather_kernel, out_shape=[on_chip((SLOTS, 2, d_model, d_ff...  16.6 us

profile of v8, /device:TPU:0, one launch (start us, length us, event | category | flops | bytes accessed | tf_op | source)
XLA Modules:
  0.0 70.4 jit_solution(17018325391595901454)
XLA Ops:
  0.0 16.6 %gather.1 = (bf16[3,2,2048,1408]{3,2,1,0:T(8,128)(2,1)S(1)}, bf16[512,2048]{1,0:T(8,128)(2,1)S(1)}, f32[8,512]{1,0:T(8,128)S(1)}, bf16[4,3,128,256]{3,2,1,0:T(8,...) custom-call(bf16[64,2048]{1,0:T(8,128)(2,1)} %tok.1, ...), custom_call_target="tpu_custom_call" | custom-call | tf_op jit(solution)/shard_map/gather/pallas_call | solution.py:379
  16.6 24.0 %hidden.1 = (bf16[3,2,2048,1408]{3,2,1,0:T(8,128)(2,1)S(1)}, bf16[8,256,1408]{2,1,0:T(8,128)(2,1)S(1)}, bf16[2,8,256,256]{3,2,1,0:T(8,128)(2,1)S(1)}) custom-call(bf16[3,2,2048,1408]{3,2,1,0:T(8,128)(2,1)S(1)} %get-tuple-element.14.w_in, ...), custom_call_target="tpu_custom_call", output_to_operand_aliasing={{0}: (0, {}), {1}: (1, {}), {2}: (2, {})} | custom-call | tf_op jit(solution)/shard_map/hidden/pallas_call | solution.py:403
  40.6 29.0 %combine.1 = bf16[64,2048]{1,0:T(8,128)(2,1)S(1)} custom-call(bf16[8,256,1408]{2,1,0:T(8,128)(2,1)S(1)} %get-tuple-element.20.h, bf16[4,3,128,256]{3,2,1,0:T(8,128)(2,1)S(1)} %get-tuple-element.21.s, bf16[2,8,256,256]{3,2,1,0:T(8,128)(2,1)S(1)} %get-tuple-element.22.o_on, bf16[8,1408,2048]{2,1,0:T(8,128)(2,1)} %wd.3), custom_call_target="tpu_custom_call" | custom-call | tf_op jit(solution)/shard_map/combine/pallas_call | solution.py:413
  69.6 0.7 %copy.14 = bf16[64,2048]{1,0:T(8,128)(2,1)} copy(bf16[64,2048]{1,0:T(8,128)(2,1)S(1)} %combine.1) | data formatting | bytes 524288

commit v9 on v5

--- a/solution.py
+++ b/solution.py
@@ -69,6 +69,7 @@
     for e in range(EARLY):
         loads.append(pltpu.make_async_copy(wg.at[e], w_out.at[e, 0], w_sem.at[e, 0]))
         loads.append(pltpu.make_async_copy(wu.at[e], w_out.at[e, 1], w_sem.at[e, 1]))
+    loads.append(pltpu.make_async_copy(wg.at[EARLY], w_out.at[EARLY, 0], w_sem.at[EARLY, 0]))
     for load in loads:
         load.start()
 
@@ -167,17 +168,15 @@
         load.wait()
 
 
-def hidden_kernel(w_in, h_in, wd_in, x_all, codes, wg, wu, wd, w_buf, h_out, wd_out, xe, w_sem, d_sem):
+def hidden_kernel(w_in, h_in, wd_in, x_all, codes, wg, wu, wd, w_buf, h_out, wd_out, xe, order, w_sem, d_sem):
     n_exp = wg.shape[0]
     d_ff = wg.shape[2]
 
-    def load(e, part, src):
-        s = lax.rem(e, SLOTS)
+    def load(n, e, part, src):
+        s = lax.rem(n, SLOTS)
         return pltpu.make_async_copy(src.at[e], w_buf.at[s, part], w_sem.at[s, part])
 
-    for e in range(EARLY, SLOTS):
-        load(e, 0, wg).start()
-        load(e, 1, wu).start()
+    load(EARLY, EARLY, 1, wu).start()
     down = pltpu.make_async_copy(wd.at[:, :, pl.ds(0, COLS)], wd_out, d_sem)
 
     def hidden_rows(e, cap, slot):
@@ -210,18 +209,34 @@
         ab = jnp.dot(rows, both, preferred_element_type=F32)
         put(act_of(ab[:, :128], ab[:, 128:]), c, 128)
 
-    def step(e, carry):
-        slot = lax.rem(e, SLOTS)
-
-        @pl.when(e >= EARLY)
-        def _():
-            load(e, 0, wg).wait()
-            load(e, 1, wu).wait()
-
-        code_row = codes[pl.ds(e, 1), :]
-        block = lax.broadcasted_iota(jnp.int32, (1, 512), 1) // 64
-        most = jnp.max(code_row - (block * CAP).astype(F32))
-        small = most <= 16.0
+    block = lax.broadcasted_iota(jnp.int32, (1, 512), 1) // 64
+
+    def few(e):
+        return jnp.max(codes[pl.ds(e, 1), :] - (block * CAP).astype(F32)) <= 16.0
+
+    for e in range(SLOTS):
+        order[e] = e
+    small_of = [few(e).astype(jnp.int32) for e in range(SLOTS, n_exp)]
+    n_large = len(small_of) - sum(small_of)
+    large_seen, small_seen = jnp.int32(0), n_large
+    for e, is_small in enumerate(small_of):
+        order[SLOTS + jnp.where(is_small == 1, small_seen, large_seen)] = e + SLOTS
+        small_seen = small_seen + is_small
+        large_seen = large_seen + 1 - is_small
+
+    def step(n, carry):
+        e = order[n]
+        slot = lax.rem(n, SLOTS)
+
+        @pl.when(n > EARLY)
+        def _():
+            load(n, e, 0, wg).wait()
+
+        @pl.when(n >= EARLY)
+        def _():
+            load(n, e, 1, wu).wait()
+
+        small = few(e)
 
         @pl.when(small)
         def _():
@@ -231,12 +246,13 @@
         def _():
             hidden_rows(e, CAP, slot)
 
-        @pl.when(e + SLOTS < n_exp)
-        def _():
-            load(e + SLOTS, 0, wg).start()
-            load(e + SLOTS, 1, wu).start()
-
-        @pl.when(e + SLOTS == n_exp)
+        @pl.when(n + SLOTS < n_exp)
+        def _():
+            following = order[jnp.minimum(n + SLOTS, n_exp - 1)]
+            load(n + SLOTS, following, 0, wg).start()
+            load(n + SLOTS, following, 1, wu).start()
+
+        @pl.when(n + SLOTS == n_exp)
         def _():
             down.start()
 
@@ -382,7 +398,7 @@
                 pltpu.VMEM((2, 8, 128), F32),
                 pltpu.VMEM((N_DEV, 16, 128), F32),
                 pltpu.VMEM((N_DEV, 16, 128), F32),
-                dma((EARLY, 2)),
+                dma((SLOTS, 2)),
                 dma((3,)),
                 dma((7,)),
                 dma((7,)),
@@ -399,7 +415,7 @@
             out_shape=[on_chip(w_on.shape, BF16), on_chip(hidden, BF16), on_chip(wd_on.shape, BF16)],
             in_specs=[VMEM] * 5 + [ANY] * 3,
             out_specs=[VMEM] * 3,
-            scratch_shapes=[pltpu.VMEM((256, d_model), BF16), dma((SLOTS, 2)), dma],
+            scratch_shapes=[pltpu.VMEM((256, d_model), BF16), pltpu.SMEM((n_exp,), jnp.int32), dma((SLOTS, 2)), dma],
             input_output_aliases={0: 0, 1: 1, 2: 2},
             compiler_params=pltpu.CompilerParams(vmem_limit_bytes=LIMIT),
             name="hidden",

time: 66.6 us -> 66.6 us (level)
    pallas_call x1, Pallas kernels: 29.1 us -> 30.7 us  [local_step(): pl.pallas_call(combine_kernel, out_shape=jax.ShapeDtypeStruct((n_tok, d_m...]
    pallas_call x1, Pallas kernels: 20 us -> 19.1 us  [local_step(): pl.pallas_call(hidden_kernel, out_shape=[on_chip(w_on.shape, BF16), on_ch...]
where the time goes in v9:
time: 66.6 us; the launch traced here: 67.1 us
  Pallas kernels  66.4 us (100%)
  local copies, waits for them, and re-layouts  0.71 us (1%)
    pallas_call x1, Pallas kernels, local_step(): pl.pallas_call(combine_kernel, out_shape=jax.ShapeDtypeStruct((n_tok, d_m...  30.7 us
    pallas_call x1, Pallas kernels, local_step(): pl.pallas_call(hidden_kernel, out_shape=[on_chip(w_on.shape, BF16), on_ch...  19.1 us
    pallas_call x1, Pallas kernels, local_step(): pl.pallas_call(gather_kernel, out_shape=[on_chip((SLOTS, 2, d_model, d_ff...  16.6 us

profile of v9, /device:TPU:0, one launch (start us, length us, event | category | flops | bytes accessed | tf_op | source)
XLA Modules:
  0.0 67.1 jit_solution(2512841730493205835)
XLA Ops:
  0.0 16.6 %gather.1 = (bf16[4,2,2048,1408]{3,2,1,0:T(8,128)(2,1)S(1)}, bf16[512,2048]{1,0:T(8,128)(2,1)S(1)}, f32[8,512]{1,0:T(8,128)S(1)}, bf16[8,256,1408]{2,1,0:T(8,128...) custom-call(bf16[64,2048]{1,0:T(8,128)(2,1)} %tok.1, s32[6,64]{1,0:T(8,128)} %bitcast.2, ...), custom_call_target="tpu_custom_call" | custom-call | tf_op jit(solution)/shard_map/gather/pallas_call | solution.py:390
  16.6 19.1 %hidden.1 = (bf16[4,2,2048,1408]{3,2,1,0:T(8,128)(2,1)S(1)}, bf16[8,256,1408]{2,1,0:T(8,128)(2,1)S(1)}, bf16[8,1408,256]{2,1,0:T(8,128)(2,1)S(1)}) custom-call(bf16[4,2,2048,1408]{3,2,1,0:T(8,128)(2,1)S(1)} %get-tuple-element.13.w_in, bf16[8,256,1408]{2,1,0:T(8,128)(2,1)S(1)} %get-tuple-element.14.h_in, ...), custom_call_target="tpu_custom_call", output_to_operand_aliasing={{0}: (0, {}), {1}: (1, {}), {2}: (2, {})} | custom-call | tf_op jit(solution)/shard_map/hidden/pallas_call | solution.py:413
  35.7 30.7 %combine.1 = bf16[64,2048]{1,0:T(8,128)(2,1)S(1)} custom-call(bf16[8,256,1408]{2,1,0:T(8,128)(2,1)S(1)} %get-tuple-element.18.h, bf16[4,3,128,256]{3,2,1,0:T(8,128)(2,1)S(1)} %get-tuple-element.19.s, bf16[8,1408,256]{2,1,0:T(8,128)(2,1)S(1)} %get-tuple-element.20.wd_on, bf16[8,1408,2048]{2,1,0:T(8,128)(2,1)} %wd.3), custom_call_target="tpu_custom_call" | custom-call | tf_op jit(solution)/shard_map/combine/pallas_call | solution.py:423
  66.4 0.7 %copy.14 = bf16[64,2048]{1,0:T(8,128)(2,1)} copy(bf16[64,2048]{1,0:T(8,128)(2,1)S(1)} %combine.1) | data formatting | bytes 524288

commit v10 on v9

--- a/solution.py
+++ b/solution.py
@@ -12,7 +12,7 @@
 CAP = 32
 SLOTS = 4
 EARLY = 3
-FRONT = 6
+FRONT = 2
 LAG_3 = 3
 LAG_4 = 6
 LIMIT = 4 << 20
@@ -271,8 +271,8 @@
     first, second = pl.ds(0, half), pl.ds(half, half)
 
     def load(b):
-        slot = lax.rem(b - 1, n_buf)
-        return pltpu.make_async_copy(wd.at[:, :, pl.ds(pl.multiple_of(b * COLS, COLS), COLS)], wd_buf.at[slot], w_sem.at[slot])
+        slot = (b - 1) % n_buf
+        return pltpu.make_async_copy(wd.at[:, :, pl.ds(b * COLS, COLS)], wd_buf.at[slot], w_sem.at[slot])
 
     load(1).start()
     barrier = pltpu.get_barrier_semaphore()
@@ -293,11 +293,6 @@
 
     def send_2b(b):
         return remote(part.at[b, core, y, 1 - x, second], h2b.at[b], h2bs.at[b], h2br.at[b], xn)
-
-    def lag(b, k, body):
-        @pl.when((b >= k) & (b < n_blk + k))
-        def _():
-            body(b - k)
 
     def stage_1(b):
         send_d2d(b).start()
@@ -319,55 +314,43 @@
     def stage_4(b):
         send_2a(b).wait_recv()
         send_2b(b).wait_recv()
-        cols = pl.ds(pl.multiple_of(b * COLS, COLS), COLS)
+        cols = pl.ds(b * COLS, COLS)
         y_out[first, cols] = (part[b, core, y, x, first] + h2a[b]).astype(BF16)
         y_out[second, cols] = (part[b, core, y, x, second] + h2b[b]).astype(BF16)
 
-    def down(e, weights):
+    def down(b, e, weights):
         out = jnp.dot(h[e], weights[e], preferred_element_type=F32).astype(BF16)
         for i in range(N_DEV):
-            o[i, pl.ds(e * CAP, CAP), :] = out[i * CAP : (i + 1) * CAP]
-
-    def front(b, weights):
-        for e in range(FRONT):
-            down(e, weights)
-
-        @pl.when(b + 2 < n_blk)
-        def _():
-            load(b + 2).start()
-
-    def back(b, weights):
-        for e in range(FRONT, n_exp):
-            down(e, weights)
+            o[b % 2, i, pl.ds(e * CAP, CAP), :] = out[i * CAP : (i + 1) * CAP]
+
+    def gather_sum(b):
         for i in range(N_DEV):
             gates = s[i // 2, :, pl.ds((i % 2) * 64, 64), :].reshape(192, 256)
-            terms = jnp.dot(gates, o[i], preferred_element_type=F32)
+            terms = jnp.dot(gates, o[b % 2, i], preferred_element_type=F32)
             part[b, i % 2, i // 4, (i // 2) % 2] = terms[0:64] + terms[64:128] + terms[128:192]
 
-    front(0, wd_on)
-    back(0, wd_on)
-    pl.semaphore_wait(barrier, N_DEV - 1)
-
-    def step(b, carry):
-        lag(b, 1, stage_1)
-        weights = wd_buf.at[lax.rem(b - 1, n_buf)]
-
-        @pl.when(b < n_blk)
-        def _():
-            load(b).wait()
-            front(b, weights)
-
-        lag(b, 1, stage_2)
-        lag(b, LAG_3, stage_3)
-        lag(b, LAG_4, stage_4)
-
-        @pl.when(b < n_blk)
-        def _():
-            back(b, weights)
-
-        return carry
-
-    lax.fori_loop(1, n_blk + LAG_4, step, 0)
+    def weights_of(b):
+        return wd_on if b == 0 else wd_buf.at[(b - 1) % n_buf]
+
+    for b in range(n_blk + LAG_4):
+        if b < n_blk:
+            if b > 0:
+                load(b).wait()
+            for e in range(FRONT):
+                down(b, e, weights_of(b))
+        if 1 <= b < n_blk + 1:
+            gather_sum(b - 1)
+            if b == 1:
+                pl.semaphore_wait(barrier, N_DEV - 1)
+            stage_1(b - 1)
+        if b < n_blk:
+            if b + 2 < n_blk:
+                load(b + 2).start()
+            for e in range(FRONT, n_exp):
+                down(b, e, weights_of(b))
+        for k, stage in ((1, stage_2), (LAG_3, stage_3), (LAG_4, stage_4)):
+            if k <= b < n_blk + k:
+                stage(b - k)
 
     def drain(b, carry):
         for send in (send_d2d, send_1a, send_1b, send_2a, send_2b):
@@ -427,7 +410,7 @@
             out_specs=VMEM,
             scratch_shapes=[
                 pltpu.VMEM((3, n_exp, d_ff, COLS), BF16),
-                pltpu.VMEM((N_DEV, 256, COLS), BF16),
+                pltpu.VMEM((2, N_DEV, 256, COLS), BF16),
                 pltpu.VMEM((n_blk, 2, 2, 2, n_tok, COLS), F32),
                 pltpu.VMEM((n_blk, 2, 2, n_tok, COLS), F32),
                 pltpu.VMEM((n_blk, 2, n_tok // 2, COLS), F32),
@@ -437,7 +420,7 @@
                 dma((3,)),
             ]
             + [dma((n_blk,))] * 10,
-            compiler_params=pltpu.CompilerParams(collective_id=1, has_side_effects=True, vmem_limit_bytes=32 << 20),
+            compiler_params=pltpu.CompilerParams(collective_id=1, has_side_effects=True, vmem_limit_bytes=33 << 20),
             name="combine",
         )(pin(h), pin(s), pin(wd_on), wd)
 

time: 66.6 us -> 67.1 us (level)
    pallas_call x1, Pallas kernels: 30.7 us -> 28.7 us  [local_step(): pl.pallas_call(combine_kernel, out_shape=jax.ShapeDtypeStruct((n_tok, d_m...]
    pallas_call x1, Pallas kernels: 19.1 us -> 21 us  [local_step(): pl.pallas_call(hidden_kernel, out_shape=[on_chip(w_on.shape, BF16), on_ch...]
where the time goes in v10:
time: 67.1 us
  Pallas kernels  66.3 us (99%)
  local copies, waits for them, and re-layouts  0.71 us (1%)
    pallas_call x1, Pallas kernels, local_step(): pl.pallas_call(combine_kernel, out_shape=jax.ShapeDtypeStruct((n_tok, d_m...  28.7 us
    pallas_call x1, Pallas kernels, local_step(): pl.pallas_call(hidden_kernel, out_shape=[on_chip(w_on.shape, BF16), on_ch...  21 us
    pallas_call x1, Pallas kernels, local_step(): pl.pallas_call(gather_kernel, out_shape=[on_chip((SLOTS, 2, d_model, d_ff...  16.6 us

profile of v10, /device:TPU:0, one launch (start us, length us, event | category | flops | bytes accessed | tf_op | source)
XLA Modules:
  0.0 67.1 jit_solution(15215461188208607649)
XLA Ops:
  0.0 16.6 %gather.1 = (bf16[4,2,2048,1408]{3,2,1,0:T(8,128)(2,1)S(1)}, bf16[512,2048]{1,0:T(8,128)(2,1)S(1)}, f32[8,512]{1,0:T(8,128)S(1)}, bf16[8,256,1408]{2,1,0:T(8,128...) custom-call(bf16[64,2048]{1,0:T(8,128)(2,1)} %tok.1, s32[6,64]{1,0:T(8,128)} %bitcast.2, ...), custom_call_target="tpu_custom_call" | custom-call | tf_op jit(solution)/shard_map/gather/pallas_call | solution.py:373
  16.6 21.0 %hidden.1 = (bf16[4,2,2048,1408]{3,2,1,0:T(8,128)(2,1)S(1)}, bf16[8,256,1408]{2,1,0:T(8,128)(2,1)S(1)}, bf16[8,1408,256]{2,1,0:T(8,128)(2,1)S(1)}) custom-call(bf16[4,2,2048,1408]{3,2,1,0:T(8,128)(2,1)S(1)} %get-tuple-element.13.w_in, bf16[8,256,1408]{2,1,0:T(8,128)(2,1)S(1)} %get-tuple-element.14.h_in, ...), custom_call_target="tpu_custom_call", output_to_operand_aliasing={{0}: (0, {}), {1}: (1, {}), {2}: (2, {})} | custom-call | tf_op jit(solution)/shard_map/hidden/pallas_call | solution.py:396
  37.7 28.7 %combine.1 = bf16[64,2048]{1,0:T(8,128)(2,1)S(1)} custom-call(bf16[8,256,1408]{2,1,0:T(8,128)(2,1)S(1)} %get-tuple-element.18.h, bf16[4,3,128,256]{3,2,1,0:T(8,128)(2,1)S(1)} %get-tuple-element.19.s, bf16[8,1408,256]{2,1,0:T(8,128)(2,1)S(1)} %get-tuple-element.20.wd_on, bf16[8,1408,2048]{2,1,0:T(8,128)(2,1)} %wd.3), custom_call_target="tpu_custom_call" | custom-call | tf_op jit(solution)/shard_map/combine/pallas_call | solution.py:406
  66.4 0.7 %copy.14 = bf16[64,2048]{1,0:T(8,128)(2,1)} copy(bf16[64,2048]{1,0:T(8,128)(2,1)S(1)} %combine.1) | data formatting | bytes 524288
